TPU v7x, 32 devices: a whole 2x2x4 slice. The times are simulated.
32 devices in a mesh: rep: 2 (over x), dp: 16 (over y, z, core).
Axes of the slice: x: 2, y: 2, z: 4, core: 2. Of those that a mesh axis runs over, the one named last changes fastest.
Arguments:
- g_w_gate: bfloat16 [32, 2, 1280, 5120], P(('rep', 'dp')), parts along dimension 0
- g_w_up: bfloat16 [32, 2, 1280, 5120], P(('rep', 'dp')), parts along dimension 0
- g_w_down: bfloat16 [32, 2, 5120, 1280], P(('rep', 'dp')), parts along dimension 0
- w_gate: bfloat16 [2, 1280, 5120], replicated
- w_up: bfloat16 [2, 1280, 5120], replicated
- w_down: bfloat16 [2, 5120, 1280], replicated
- m_w_gate: float32 [2, 1280, 5120], P(None, 'dp')
- m_w_up: float32 [2, 1280, 5120], P(None, 'dp')
- m_w_down: float32 [2, 5120, 1280], P(None, 'dp')
- v_w_gate: float32 [2, 1280, 5120], P(None, 'dp')
- v_w_up: float32 [2, 1280, 5120], P(None, 'dp')
- v_w_down: float32 [2, 5120, 1280], P(None, 'dp')
Outputs:
- output 1: bfloat16 [4, 1280, 5120], P('rep'), parts along dimension 0
- output 2: bfloat16 [4, 1280, 5120], P('rep'), parts along dimension 0
- output 3: bfloat16 [4, 5120, 1280], P('rep'), parts along dimension 0
- output 4: float32 [4, 1280, 5120], P('rep', 'dp'), parts along dimension 0
- output 5: float32 [4, 1280, 5120], P('rep', 'dp'), parts along dimension 0
- output 6: float32 [4, 5120, 1280], P('rep', 'dp'), parts along dimension 0
- output 7: float32 [4, 1280, 5120], P('rep', 'dp'), parts along dimension 0
- output 8: float32 [4, 1280, 5120], P('rep', 'dp'), parts along dimension 0
- output 9: float32 [4, 5120, 1280], P('rep', 'dp'), parts along dimension 0
There are 2 independent parts. A program takes and returns all parts, laid end to end along the dimension named above; an argument that names none is the same for every part.
All inputs are finite; a program needn't handle non-finite values.
Results may differ from a plain program's by a relative error of at most 0.022.
Values are sent between devices in bfloat16 or wider.
A program may use at most 2 GiB of HBM per device.

v0:
```python
import functools

import jax
import jax.numpy as jnp
from jax import lax
from jax.experimental import pallas as pl
from jax.experimental.pallas import tpu as pltpu
from jax.sharding import PartitionSpec as P

MESH = pl.DeviceIdType.MESH
BF16, F32 = jnp.bfloat16, jnp.float32
CHIPS = 8
HOPS = 5
VMEM_LIMIT = 60 * 1024 * 1024
SLOTS, LAG = 8, 4
ROWS = 16
COLS = 1280


def moments(m, v, g):
    return 0.9 * m + 0.1 * g, 0.95 * v + 0.05 * g * g


def adamw(w, m, v, g):
    m, v = moments(m, v, g)
    step = m * lax.rsqrt(v + 1e-8) + 0.1 * w
    return (w - 0.02 * step).astype(BF16)


def ring_place(chip):
    return lax.select(chip < 4, chip, 11 - chip)


def each_tile(shape, body):
    rows, cols = shape

    def one(i, _):
        for c in range(cols // COLS):
            body(pl.ds(pl.multiple_of(i * ROWS, ROWS), ROWS), pl.ds(c * COLS, COLS))
        return 0

    lax.fori_loop(0, rows // ROWS, one, 0)


def step_kernel(sizes, *refs):
    n = len(sizes)
    refs = list(refs)

    def take(count):
        taken = refs[:count]
        del refs[:count]
        return taken

    terms, weights, old_m, old_v = take(n), take(n), take(n), take(n)
    sums, edges, (factor_ref,), whole, lent, ring = take(n), take(n), take(1), take(n), take(n), take(n)
    own, other, came, held, final, m_in, v_in = (take(n) for _ in range(7))
    acc, totals, lend_s, lend_r, ring_s, ring_r, load_own, load_other, load_came, load_m, load_v, store, norm_s, norm_r = refs

    me = lax.axis_index("dp")
    core, chip = lax.rem(me, 2), lax.div(me, 2)
    place = ring_place(chip)
    way = 1 - 2 * core
    partner = chip * 2 + 1 - core
    following = ring_place(lax.rem(place + way + CHIPS, CHIPS)) * 2 + core
    jobs = [(k, layer) for k in range(n) for layer in range(2)]
    every = range(len(jobs))

    def rows_of(k, block):
        return pl.ds(pl.multiple_of(block * sizes[k][0], 16), sizes[k][0])

    def block_at(step, c):
        at = lax.rem(place - (1 - 2 * c) * (1 + step) + 2 * CHIPS, CHIPS)
        return ring_place(at) * 2 + c

    def remote(src, dst, send, recv, to):
        return pltpu.make_async_remote_copy(
            src_ref=src, dst_ref=dst, send_sem=send, recv_sem=recv, device_id={"dp": to}, device_id_type=MESH
        )

    def lend(step, j):
        k, layer = jobs[j]
        src = terms[k].at[layer, rows_of(k, block_at(step, 1 - core))]
        return remote(src, lent[k].at[step, layer], lend_s.at[j], lend_r.at[step, j], partner)

    def pass_on(step, j):
        k, layer = jobs[j]
        return remote(held[k].at[layer], ring[k].at[step, layer], ring_s.at[j], ring_r.at[step, j], following)

    def get_own(step, j):
        k, layer = jobs[j]
        return pltpu.make_async_copy(terms[k].at[layer, rows_of(k, block_at(step, core))], own[k].at[layer], load_own.at[j])

    def get_other(step, j):
        k, layer = jobs[j]
        return pltpu.make_async_copy(lent[k].at[step, layer], other[k].at[layer], load_other.at[j])

    def get_came(step, j):
        k, layer = jobs[j]
        return pltpu.make_async_copy(ring[k].at[step, layer], came[k].at[layer], load_came.at[j])

    def get_state(j):
        k, layer = jobs[j]
        return (
            pltpu.make_async_copy(old_m[k].at[layer], m_in[k].at[layer], load_m.at[j]),
            pltpu.make_async_copy(old_v[k].at[layer], v_in[k].at[layer], load_v.at[j]),
        )

    def get_weight(j):
        k, layer = jobs[j]
        return pltpu.make_async_copy(weights[k].at[layer, rows_of(k, me)], came[k].at[layer], load_came.at[j])

    def put_sum(j):
        k, layer = jobs[j]
        return pltpu.make_async_copy(final[k].at[layer], sums[k].at[layer], load_own.at[j])

    barrier = pltpu.get_barrier_semaphore()

    def greet(i, _):
        pl.semaphore_signal(barrier, inc=1, device_id={"dp": lax.rem(me + i, 16)}, device_id_type=MESH)
        return 0

    lax.fori_loop(1, 16, greet, 0)
    for j in every:
        get_own(0, j).start()
    acc[...] = jnp.zeros_like(acc)
    pl.semaphore_wait(barrier, 15)
    for j in every:
        lend(0, j).start()

    def one(step, j, first, last):
        k, layer = jobs[j]
        a, b, c, h = (ref[k].at[layer] for ref in (own, other, came, final if last else held))
        lend(step, j).wait_recv()
        get_other(step, j).start()
        if not first:
            pass_on(step - 1, j).wait_recv()
            get_came(step - 1, j).start()
        lend(step, j).wait_send()
        if not last:
            lend(step + 1, j).start()
        if not first:
            pass_on(step - 1, j).wait_send()
        get_own(step, j).wait()
        get_other(step, j).wait()
        if not first:
            get_came(step - 1, j).wait()

        def add(r, c_):
            so_far = a[r, c_].astype(F32) + b[r, c_].astype(F32)
            if not first:
                so_far = so_far + c[r, c_].astype(F32)
            rounded = so_far.astype(BF16)
            h[r, c_] = rounded
            if last:
                g = rounded.astype(F32)
                acc[...] += g * g

        each_tile(sizes[k], add)
        if not last:
            pass_on(step, j).start()
            get_own(step + 1, j).start()
        else:
            get_weight(j).start()
            put_sum(j).start()

    for j in every:
        one(0, j, True, False)
    for j in every:
        for copy in get_state(j):
            copy.start()

    def middle(step, _):
        for j in every:
            one(step, j, False, False)
        return 0

    lax.fori_loop(1, CHIPS - 1, middle, 0)
    for j in every:
        one(CHIPS - 1, j, False, True)

    mine = jnp.zeros((8, 128), F32)
    for r in range(ROWS // 8):
        for c in range(COLS // 128):
            mine = mine + acc[r * 8 : r * 8 + 8, c * 128 : c * 128 + 128]
    totals[me] = mine

    def tell(i):
        return remote(totals.at[me], totals.at[me], norm_s.at[i], norm_r.at[i], lax.rem(me + i, 16))

    for i in range(1, 16):
        tell(i).start()
    for j in every:
        get_weight(j).wait()
        for copy in get_state(j):
            copy.wait()
    for i in range(1, 16):
        tell(i).wait()
    total = totals[0]
    for i in range(1, 16):
        total = total + totals[i]
    count = 16 * 2 * sum(rows * cols for rows, cols in sizes)
    factor_ref[...] = jnp.minimum(1.0, 0.5 * lax.rsqrt(jnp.full((8, 128), jnp.sum(total)) / count + 1e-30))
    factor = jnp.max(factor_ref[...])

    def rows_at(k, h):
        return rows_of(k, ring_place(lax.rem(place - way * h + CHIPS, CHIPS)) * 2 + core)

    def block_of(h, j):
        k, layer = jobs[j]
        first = isinstance(h, int) and h == 0
        return held[k].at[layer] if first else whole[k].at[layer, rows_at(k, h)]

    def hop(h, j, to_edge=False):
        k, layer = jobs[j]
        dst = edges[k].at[layer] if to_edge else whole[k].at[layer, rows_at(k, h)]
        return remote(block_of(h, j), dst, ring_s.at[j], ring_r.at[h, j], following)

    def give(h, j):
        k, layer = jobs[j]
        return remote(block_of(h, j), whole[k].at[layer, rows_at(k, h)], lend_s.at[j], lend_r.at[h, j], partner)

    def keep(j):
        k, layer = jobs[j]
        return pltpu.make_async_copy(block_of(0, j), whole[k].at[layer, rows_at(k, 0)], store.at[j])

    for j in every:
        k, layer = jobs[j]
        a, w, m, v, h = (ref[k].at[layer] for ref in (final, came, m_in, v_in, held))

        def update(r, c_):
            h[r, c_] = adamw(w[r, c_].astype(F32), m[r, c_], v[r, c_], a[r, c_].astype(F32) * factor)

        each_tile(sizes[k], update)
        hop(0, j).start()
        give(0, j).start()
        keep(j).start()

    def along(h, _):
        for j in every:
            hop(h - 1, j).wait()
            hop(h, j).start()
            give(h - 1, j).wait()
            give(h, j).start()
        return 0

    lax.fori_loop(1, HOPS - 1, along, 0)
    last = HOPS - 1
    for j in every:
        hop(last - 1, j).wait()
        hop(last, j, True).start()
        give(last - 1, j).wait()
        give(last, j).start()
    for j in every:
        keep(j).wait()
        put_sum(j).wait()
        give(last, j).wait()
    for j in every:
        hop(last, j, True).wait()


def step_call(terms, weights, m, v):
    n = len(terms)
    sizes = tuple(one.shape[1:] for one in m)
    hbm, vmem = pl.BlockSpec(memory_space=pltpu.HBM), pl.BlockSpec(memory_space=pltpu.VMEM)
    arrays = lambda count: [jax.ShapeDtypeStruct((*count, 2, *s), BF16) for s in sizes]
    buffers = lambda kind: [pltpu.VMEM((2, *s), kind) for s in sizes]
    dma = pltpu.SemaphoreType.DMA
    jobs = 2 * n
    out = pl.pallas_call(
        functools.partial(step_kernel, sizes),
        out_shape=[
            *arrays(()),
            *arrays(()),
            jax.ShapeDtypeStruct((8, 128), F32),
            *(jax.ShapeDtypeStruct(w.shape, BF16) for w in weights),
            *arrays((CHIPS,)),
            *arrays((CHIPS - 1,)),
        ],
        in_specs=[hbm] * (4 * n),
        out_specs=[hbm] * (2 * n) + [vmem] + [hbm] * (3 * n),
        scratch_shapes=[
            *buffers(BF16) * 5,
            *buffers(F32) * 2,
            pltpu.VMEM((ROWS, COLS), F32),
            pltpu.VMEM((16, 8, 128), F32),
            dma((jobs,)),
            dma((CHIPS, jobs)),
            dma((jobs,)),
            dma((CHIPS - 1, jobs)),
            *[dma((jobs,))] * 6,
            dma((16,)),
            dma((16,)),
        ],
        compiler_params=pltpu.CompilerParams(collective_id=0, has_side_effects=True, vmem_limit_bytes=VMEM_LIMIT),
        cost_estimate=pl.CostEstimate(flops=400_000_000, bytes_accessed=300_000_000, transcendentals=0),
        name="step_kernel",
    )(*terms, *weights, *m, *v)
    return out[:n], out[n : 2 * n], out[2 * n][0, 0], out[2 * n + 1 : 3 * n + 1]


def move(tasks, slots, load, store):
    def read(t):
        return pltpu.make_async_copy(tasks[t][0], slots.at[t % SLOTS], load.at[t % SLOTS])

    def write(t):
        return pltpu.make_async_copy(slots.at[t % SLOTS], tasks[t][1], store.at[t % SLOTS])

    count = len(tasks)
    for t in range(count + LAG):
        if t < count:
            if t >= SLOTS:
                write(t - SLOTS).wait()
            read(t).start()
        if t >= LAG:
            read(t - LAG).wait()
            write(t - LAG).start()
    for t in range(max(0, count - SLOTS), count):
        write(t).wait()


def rows_back(h, rows, mine):
    me = lax.axis_index("dp")
    core, place = lax.rem(me, 2), ring_place(lax.div(me, 2))
    of = core if mine else 1 - core
    block = ring_place(lax.rem(place - (1 - 2 * of) * h + CHIPS, CHIPS)) * 2 + of
    return pl.ds(pl.multiple_of(block * rows, 16), rows)


def fill_kernel(rows, whole, edge, edge_given, came, given, out, slots, load, store):
    tasks = []
    for layer in range(2):
        for mine in (True, False):
            for h in range(HOPS):
                at = out.at[layer, rows_back(h, rows, mine)]
                tasks.append((whole.at[layer, rows_back(h, rows, mine)], at))
        for h, mine, src in ((HOPS, True, edge), (HOPS, False, edge_given), (HOPS + 1, True, came), (HOPS + 1, False, given)):
            tasks.append((src.at[layer], out.at[layer, rows_back(h, rows, mine)]))
    move(tasks, slots, load, store)


def finish_kernel(rows, _, came, given, out, slots, load, store):
    tasks = []
    for layer in range(2):
        for mine, src in ((True, came), (False, given)):
            tasks.append((src.at[layer], out.at[layer, rows_back(HOPS + 2, rows, mine)]))
    move(tasks, slots, load, store)


def local_call(kernel, arrays, block, aliases, flops):
    hbm = pl.BlockSpec(memory_space=pltpu.HBM)
    return pl.pallas_call(
        functools.partial(kernel, block[0]),
        out_shape=jax.ShapeDtypeStruct(arrays[0].shape, BF16),
        in_specs=[hbm] * len(arrays),
        out_specs=hbm,
        input_output_aliases=aliases,
        scratch_shapes=[
            pltpu.VMEM((SLOTS, *block), BF16),
            pltpu.SemaphoreType.DMA((SLOTS,)),
            pltpu.SemaphoreType.DMA((SLOTS,)),
        ],
        compiler_params=pltpu.CompilerParams(vmem_limit_bytes=VMEM_LIMIT),
        cost_estimate=pl.CostEstimate(flops=flops, bytes_accessed=arrays[0].size * 4, transcendentals=0),
    )(*arrays)


def permute(arrays, pairs):
    out = []
    for one in arrays:
        out.append(lax.ppermute(one, "dp", pairs))
    return out


def solution(mesh):
    place = lambda chip: chip if chip < 4 else 11 - chip
    onward = [(2 * q + c, 2 * place((place(q) + 1 - 2 * c) % CHIPS) + c) for q in range(CHIPS) for c in range(2)]
    across = [(i, i ^ 1) for i in range(2 * CHIPS)]

    def step(*arrays):
        terms, weights, m, v = (arrays[i : i + 3] for i in (0, 3, 6, 9))
        sums, edges, factor, gathered = step_call([t[0] for t in terms], weights, m, v)
        came = permute(edges, onward)
        last = permute(came, onward)
        edge_given, given = permute(edges, across), permute(came, across)
        last_given = permute(last, across)
        new = [moments(a, b, g.astype(F32) * factor) for a, b, g in zip(m, v, sums, strict=True)]
        whole = []
        for k, one in enumerate(m):
            block = one.shape[1:]
            w = local_call(fill_kernel, (gathered[k], edges[k], edge_given[k], came[k], given[k]), block, {}, 60_000_000)
            whole.append(local_call(finish_kernel, (w, last[k], last_given[k]), block, {0: 0}, 8_000_000))
        return (*whole, *(one[0] for one in new), *(one[1] for one in new))

    all_of, cut = P(None, None, None), P(None, "dp", None)
    return jax.shard_map(
        step,
        mesh=mesh,
        in_specs=(P(("rep", "dp"), None, None, None),) * 3 + (all_of,) * 3 + (cut,) * 6,
        out_specs=(P("rep", None, None),) * 3 + (P("rep", "dp", None),) * 6,
        check_vma=False,
    )
```

profile of v0, /device:TPU:0, one launch (start us, length us, event | category | flops | bytes accessed | tf_op | source)
XLA Modules:
  0.0 833.7 jit_solution(15322216615131905669)
XLA Ops:
  0.6 0.0 copy-start
  0.7 655.5 %step_kernel.1 = (bf16[2,80,5120]{2,1,0:T(8,128)(2,1)}, bf16[2,80,5120]{2,1,0:T(8,128)(2,1)}, bf16[2,320,1280]{2,1,0:T(8,128)(2,1)}, bf16[2,80,5120]{2,1,0:T(8,1...) custom-call(bf16[2,1280,5120]{2,1,0:T(8,128)(2,1)} %bitcast.4, ...), custom_call_target="tpu_custom_call" | custom-call | flops 400000000 | bytes 300000000 | tf_op jit(solution)/shard_map/step_kernel/pallas_call | solution.py:269
  656.2 0.9 collective-permute-start.1
  657.1 0.0 collective-permute-start
  657.1 0.6 collective-permute-start.6
  657.7 0.7 collective-permute-start.5
  658.5 0.9 collective-permute-start.11
  659.3 18.2 %collective-permute-done.1.came = bf16[2,80,5120]{2,1,0:T(8,128)(2,1)S(1)} collective-permute-done((bf16[2,80,5120]{2,1,0:T(8,128)(2,1)}, bf16[2,80,5120]{2,1,0:T(8,128)(2,1)S(1)}, u32[]{:S(2)}, u32[]{:S(2)}) %collective-permute-start.1) | collective-permute-done | bytes 1638432 | tf_op jit(solution)/shard_map/ppermute | solution.py:370
  677.5 0.9 collective-permute-start.3
  678.4 0.0 collective-permute-done.edge_given
  678.4 0.0 collective-permute-start.2
  678.4 16.7 %collective-permute-done.6.came = bf16[2,80,5120]{2,1,0:T(8,128)(2,1)S(1)} collective-permute-done((bf16[2,80,5120]{2,1,0:T(8,128)(2,1)}, bf16[2,80,5120]{2,1,0:T(8,128)(2,1)S(1)}, u32[]{:S(2)}, u32[]{:S(2)}) %collective-permute-start.6) | collective-permute-done | bytes 1638432 | tf_op jit(solution)/shard_map/ppermute | solution.py:370
  695.1 0.9 collective-permute-start.8
  696.0 0.0 collective-permute-done.5.edge_given
  696.0 0.0 collective-permute-start.7
  696.0 16.8 %collective-permute-done.11.came = bf16[2,320,1280]{2,1,0:T(8,128)(2,1)} collective-permute-done((bf16[2,320,1280]{2,1,0:T(8,128)(2,1)}, bf16[2,320,1280]{2,1,0:T(8,128)(2,1)}, u32[]{:S(2)}, u32[]{:S(2)}) %collective-permute-start.11) | collective-permute-done | bytes 1638432 | tf_op jit(solution)/shard_map/ppermute | solution.py:370
  712.7 0.9 collective-permute-start.13
  713.6 1.2 slice.3
  714.8 0.0 copy-done
  714.8 0.0 copy-start.4
  714.8 7.6 fusion.2
  722.4 0.0 copy-done.7
  722.4 0.0 copy-done.8
  722.4 7.9 collective-permute-done.3.came
  730.3 0.0 collective-permute-start.10
  730.3 0.0 collective-permute-done.2.given
  730.3 0.5 collective-permute-start.12
  730.8 17.0 %collective-permute-done.8.came = bf16[2,80,5120]{2,1,0:T(8,128)(2,1)} collective-permute-done((bf16[2,80,5120]{2,1,0:T(8,128)(2,1)S(1)}, bf16[2,80,5120]{2,1,0:T(8,128)(2,1)}, u32[]{:S(2)}, u32[]{:S(2)}) %collective-permute-start.8) | collective-permute-done | bytes 1638432 | tf_op jit(solution)/shard_map/ppermute | solution.py:370
  747.9 0.0 collective-permute-start.4
  747.9 0.0 collective-permute-done.7.given
  747.9 0.5 collective-permute-start.9
  748.4 17.0 %collective-permute-done.13.came = bf16[2,320,1280]{2,1,0:T(8,128)(2,1)} collective-permute-done((bf16[2,320,1280]{2,1,0:T(8,128)(2,1)}, bf16[2,320,1280]{2,1,0:T(8,128)(2,1)}, u32[]{:S(2)}, u32[]{:S(2)}) %collective-permute-start.13) | collective-permute-done | bytes 1638432 | tf_op jit(solution)/shard_map/ppermute | solution.py:370
  765.4 0.0 collective-permute-start.14
  765.4 0.0 copy-done.2
  765.4 7.5 fusion
  773.0 16.7 %shard_map.187._ = bf16[2,1280,5120]{2,1,0:T(8,128)(2,1)} custom-call(bf16[2,1280,5120]{2,1,0:T(8,128)(2,1)} %get-tuple-element.19.whole, bf16[2,80,5120]{2,1,0:T(8,128)(2,1)} %get-tuple-element.20.edge, bf16[2,80,5120]{2,1,0:T(8,128)(2,1)} %copy-done.7, bf16[2,80,5120]{2,1,0:T(8,128)(2,1)} %copy-done.5, bf16[2,80,5120]{2,1,0:T(8,128)(2,1)} %copy-done.9), custom_call_target="tpu_custom_call" | custom-call | flops 60000000 | bytes 52428800 | tf_op jit(solution)/shard_map/pallas_call | solution.py:351
  789.6 16.7 %shard_map.189._ = bf16[2,1280,5120]{2,1,0:T(8,128)(2,1)} custom-call(bf16[2,1280,5120]{2,1,0:T(8,128)(2,1)} %get-tuple-element.21.whole, bf16[2,80,5120]{2,1,0:T(8,128)(2,1)} %get-tuple-element.22.edge, bf16[2,80,5120]{2,1,0:T(8,128)(2,1)} %copy-done.8, bf16[2,80,5120]{2,1,0:T(8,128)(2,1)} %copy-done.6, bf16[2,80,5120]{2,1,0:T(8,128)(2,1)} %copy-done.10), custom_call_target="tpu_custom_call" | custom-call | flops 60000000 | bytes 52428800 | tf_op jit(solution)/shard_map/pallas_call | solution.py:351
  806.3 0.0 collective-permute-done.10.edge_given
  806.3 0.0 collective-permute-done.12.given
  806.3 1.1 copy-done.11
  807.5 0.5 copy-done.12
  808.0 16.6 %shard_map.191._ = bf16[2,5120,1280]{2,1,0:T(8,128)(2,1)} custom-call(bf16[2,5120,1280]{2,1,0:T(8,128)(2,1)} %get-tuple-element.23.whole, bf16[2,320,1280]{2,1,0:T(8,128)(2,1)} %get-tuple-element.24.edge, bf16[2,320,1280]{2,1,0:T(8,128)(2,1)} %copy-done.11, bf16[2,320,1280]{2,1,0:T(8,128)(2,1)} %collective-permute-done.11.came, bf16[2,320,1280]{2,1,0:T(8,128)(2,1)} %copy-done.12), custom_call_target="tpu_custom_call" | custom-call | flops 60000000 | bytes 52428800 | tf_op jit(solution)/shard_map/pallas_call | solution.py:351
  824.7 0.0 collective-permute-done.4.given
  824.7 3.0 shard_map.188
  827.7 0.0 collective-permute-done.9.given
  827.7 3.0 shard_map.190
  830.7 0.0 collective-permute-done.14.given
  830.7 3.0 shard_map.192
  (18 shorter events, 0.0 us)
Async XLA Ops:
  0.6 714.2 %copy-start = (f32[2,320,1280]{2,1,0:T(8,128)S(1)}, f32[2,320,1280]{2,1,0:T(8,128)}, u32[]{:S(2)}) copy-start(f32[2,320,1280]{2,1,0:T(8,128)} %refs_8_.1) | copy-start | bytes 9830404
  656.2 21.4 %collective-permute-start.1 = (bf16[2,80,5120]{2,1,0:T(8,128)(2,1)}, bf16[2,80,5120]{2,1,0:T(8,128)(2,1)S(1)}, u32[]{:S(2)}, u32[]{:S(2)}) collective-permute-start(bf16[2,80,5120]{2,1,0:T(8,128)(2,1)} %get-tuple-element.20.edge), channel_id=1, source_target_pairs={{0,2},{1,9},{2,4},{3,1},{4,6},{5,3},{6,14},{7,5},{8,0},{9,11},{10,... | collective-permute-start | bytes 4915208 | tf_op jit(solution)/shard_map/ppermute | solution.py:370
  657.1 21.3 %collective-permute-start = (bf16[2,80,5120]{2,1,0:T(8,128)(2,1)}, bf16[2,80,5120]{2,1,0:T(8,128)(2,1)S(1)}, u32[]{:S(2)}, u32[]{:S(2)}) collective-permute-start(bf16[2,80,5120]{2,1,0:T(8,128)(2,1)} %get-tuple-element.20.edge), channel_id=1, source_target_pairs={{0,1},{1,0},{2,3},{3,2},{4,5},{5,4},{6,7},{7,6},{8,9},{9,8},{10,11... | collective-permute-start | bytes 4915208 | tf_op jit(solution)/shard_map/ppermute | solution.py:370
  657.1 38.0 %collective-permute-start.6 = (bf16[2,80,5120]{2,1,0:T(8,128)(2,1)}, bf16[2,80,5120]{2,1,0:T(8,128)(2,1)S(1)}, u32[]{:S(2)}, u32[]{:S(2)}) collective-permute-start(bf16[2,80,5120]{2,1,0:T(8,128)(2,1)} %get-tuple-element.22.edge), channel_id=1, source_target_pairs={{0,2},{1,9},{2,4},{3,1},{4,6},{5,3},{6,14},{7,5},{8,0},{9,11},{10,... | collective-permute-start | bytes 4915208 | tf_op jit(solution)/shard_map/ppermute | solution.py:370
  657.7 38.2 %collective-permute-start.5 = (bf16[2,80,5120]{2,1,0:T(8,128)(2,1)}, bf16[2,80,5120]{2,1,0:T(8,128)(2,1)S(1)}, u32[]{:S(2)}, u32[]{:S(2)}) collective-permute-start(bf16[2,80,5120]{2,1,0:T(8,128)(2,1)} %get-tuple-element.22.edge), channel_id=1, source_target_pairs={{0,1},{1,0},{2,3},{3,2},{4,5},{5,4},{6,7},{7,6},{8,9},{9,8},{10,11... | collective-permute-start | bytes 4915208 | tf_op jit(solution)/shard_map/ppermute | solution.py:370
  658.5 54.3 %collective-permute-start.11 = (bf16[2,320,1280]{2,1,0:T(8,128)(2,1)}, bf16[2,320,1280]{2,1,0:T(8,128)(2,1)}, u32[]{:S(2)}, u32[]{:S(2)}) collective-permute-start(bf16[2,320,1280]{2,1,0:T(8,128)(2,1)} %get-tuple-element.24.edge), channel_id=1, source_target_pairs={{0,2},{1,9},{2,4},{3,1},{4,6},{5,3},{6,14},{7,5},{8,0},{9,11},{10,... | collective-permute-start | bytes 4915208 | tf_op jit(solution)/shard_map/ppermute | solution.py:370
  677.5 44.9 %copy-start.5 = (bf16[2,80,5120]{2,1,0:T(8,128)(2,1)}, bf16[2,80,5120]{2,1,0:T(8,128)(2,1)S(1)}, u32[]{:S(2)}) copy-start(bf16[2,80,5120]{2,1,0:T(8,128)(2,1)S(1)} %collective-permute-done.1.came) | copy-start | bytes 4915204
  677.5 52.8 %collective-permute-start.3 = (bf16[2,80,5120]{2,1,0:T(8,128)(2,1)S(1)}, bf16[2,80,5120]{2,1,0:T(8,128)(2,1)}, u32[]{:S(2)}, u32[]{:S(2)}) collective-permute-start(bf16[2,80,5120]{2,1,0:T(8,128)(2,1)S(1)} %collective-permute-done.1.came), channel_id=1, source_target_pairs={{0,2},{1,9},{2,4},{3,1},{4,6},{5,3},{6,14},{7,5},{8,0},{9,11},{10,... | collective-permute-start | bytes 4915208 | tf_op jit(solution)/shard_map/ppermute | solution.py:370
  678.4 44.0 %copy-start.7 = (bf16[2,80,5120]{2,1,0:T(8,128)(2,1)}, bf16[2,80,5120]{2,1,0:T(8,128)(2,1)S(1)}, u32[]{:S(2)}) copy-start(bf16[2,80,5120]{2,1,0:T(8,128)(2,1)S(1)} %collective-permute-done.edge_given) | copy-start | bytes 4915204
  678.4 51.9 %collective-permute-start.2 = (bf16[2,80,5120]{2,1,0:T(8,128)(2,1)S(1)}, bf16[2,80,5120]{2,1,0:T(8,128)(2,1)S(1)}, u32[]{:S(2)}, u32[]{:S(2)}) collective-permute-start(bf16[2,80,5120]{2,1,0:T(8,128)(2,1)S(1)} %collective-permute-done.1.came), channel_id=1, source_target_pairs={{0,1},{1,0},{2,3},{3,2},{4,5},{5,4},{6,7},{7,6},{8,9},{9,8},{10,11... | collective-permute-start | bytes 4915208 | tf_op jit(solution)/shard_map/ppermute | solution.py:370
  695.1 27.3 %copy-start.6 = (bf16[2,80,5120]{2,1,0:T(8,128)(2,1)}, bf16[2,80,5120]{2,1,0:T(8,128)(2,1)S(1)}, u32[]{:S(2)}) copy-start(bf16[2,80,5120]{2,1,0:T(8,128)(2,1)S(1)} %collective-permute-done.6.came) | copy-start | bytes 4915204
  695.1 52.8 %collective-permute-start.8 = (bf16[2,80,5120]{2,1,0:T(8,128)(2,1)S(1)}, bf16[2,80,5120]{2,1,0:T(8,128)(2,1)}, u32[]{:S(2)}, u32[]{:S(2)}) collective-permute-start(bf16[2,80,5120]{2,1,0:T(8,128)(2,1)S(1)} %collective-permute-done.6.came), channel_id=1, source_target_pairs={{0,2},{1,9},{2,4},{3,1},{4,6},{5,3},{6,14},{7,5},{8,0},{9,11},{10,... | collective-permute-start | bytes 4915208 | tf_op jit(solution)/shard_map/ppermute | solution.py:370
  696.0 26.4 %copy-start.8 = (bf16[2,80,5120]{2,1,0:T(8,128)(2,1)}, bf16[2,80,5120]{2,1,0:T(8,128)(2,1)S(1)}, u32[]{:S(2)}) copy-start(bf16[2,80,5120]{2,1,0:T(8,128)(2,1)S(1)} %collective-permute-done.5.edge_given) | copy-start | bytes 4915204
  696.0 51.9 %collective-permute-start.7 = (bf16[2,80,5120]{2,1,0:T(8,128)(2,1)S(1)}, bf16[2,80,5120]{2,1,0:T(8,128)(2,1)S(1)}, u32[]{:S(2)}, u32[]{:S(2)}) collective-permute-start(bf16[2,80,5120]{2,1,0:T(8,128)(2,1)S(1)} %collective-permute-done.6.came), channel_id=1, source_target_pairs={{0,1},{1,0},{2,3},{3,2},{4,5},{5,4},{6,7},{7,6},{8,9},{9,8},{10,11... | collective-permute-start | bytes 4915208 | tf_op jit(solution)/shard_map/ppermute | solution.py:370
  712.7 52.7 %collective-permute-start.13 = (bf16[2,320,1280]{2,1,0:T(8,128)(2,1)}, bf16[2,320,1280]{2,1,0:T(8,128)(2,1)}, u32[]{:S(2)}, u32[]{:S(2)}) collective-permute-start(bf16[2,320,1280]{2,1,0:T(8,128)(2,1)} %collective-permute-done.11.came), channel_id=1, source_target_pairs={{0,2},{1,9},{2,4},{3,1},{4,6},{5,3},{6,14},{7,5},{8,0},{9,11},{10,... | collective-permute-start | bytes 4915208 | tf_op jit(solution)/shard_map/ppermute | solution.py:370
  714.8 50.6 %copy-start.1 = (f32[2,80,5120]{2,1,0:T(8,128)S(1)}, f32[2,80,5120]{2,1,0:T(8,128)}, u32[]{:S(2)}) copy-start(f32[2,80,5120]{2,1,0:T(8,128)} %refs_6_.1) | copy-start | bytes 9830404
  714.8 50.6 %copy-start.2 = (f32[2,80,5120]{2,1,0:T(8,128)S(1)}, f32[2,80,5120]{2,1,0:T(8,128)}, u32[]{:S(2)}) copy-start(f32[2,80,5120]{2,1,0:T(8,128)} %refs_7_.1) | copy-start | bytes 9830404
  714.8 50.6 %copy-start.3 = (f32[2,80,5120]{2,1,0:T(8,128)S(1)}, f32[2,80,5120]{2,1,0:T(8,128)}, u32[]{:S(2)}) copy-start(f32[2,80,5120]{2,1,0:T(8,128)} %refs_9_.1) | copy-start | bytes 9830404
  714.8 50.6 %copy-start.4 = (f32[2,80,5120]{2,1,0:T(8,128)S(1)}, f32[2,80,5120]{2,1,0:T(8,128)}, u32[]{:S(2)}) copy-start(f32[2,80,5120]{2,1,0:T(8,128)} %refs_10_.1) | copy-start | bytes 9830404
  730.3 76.0 %collective-permute-start.10 = (bf16[2,320,1280]{2,1,0:T(8,128)(2,1)}, bf16[2,320,1280]{2,1,0:T(8,128)(2,1)S(1)}, u32[]{:S(2)}, u32[]{:S(2)}) collective-permute-start(bf16[2,320,1280]{2,1,0:T(8,128)(2,1)} %get-tuple-element.24.edge), channel_id=1, source_target_pairs={{0,1},{1,0},{2,3},{3,2},{4,5},{5,4},{6,7},{7,6},{8,9},{9,8},{10,11... | collective-permute-start | bytes 4915208 | tf_op jit(solution)/shard_map/ppermute | solution.py:370
  730.3 42.6 %copy-start.9 = (bf16[2,80,5120]{2,1,0:T(8,128)(2,1)}, bf16[2,80,5120]{2,1,0:T(8,128)(2,1)S(1)}, u32[]{:S(2)}) copy-start(bf16[2,80,5120]{2,1,0:T(8,128)(2,1)S(1)} %collective-permute-done.2.given) | copy-start | bytes 4915204
  730.3 76.0 %collective-permute-start.12 = (bf16[2,320,1280]{2,1,0:T(8,128)(2,1)}, bf16[2,320,1280]{2,1,0:T(8,128)(2,1)S(1)}, u32[]{:S(2)}, u32[]{:S(2)}) collective-permute-start(bf16[2,320,1280]{2,1,0:T(8,128)(2,1)} %collective-permute-done.11.came), channel_id=1, source_target_pairs={{0,1},{1,0},{2,3},{3,2},{4,5},{5,4},{6,7},{7,6},{8,9},{9,8},{10,11... | collective-permute-start | bytes 4915208 | tf_op jit(solution)/shard_map/ppermute | solution.py:370
  747.9 76.8 %collective-permute-start.4 = (bf16[2,80,5120]{2,1,0:T(8,128)(2,1)}, bf16[2,80,5120]{2,1,0:T(8,128)(2,1)}, u32[]{:S(2)}, u32[]{:S(2)}) collective-permute-start(bf16[2,80,5120]{2,1,0:T(8,128)(2,1)} %collective-permute-done.3.came), channel_id=1, source_target_pairs={{0,1},{1,0},{2,3},{3,2},{4,5},{5,4},{6,7},{7,6},{8,9},{9,8},{10,11... | collective-permute-start | bytes 4915208 | tf_op jit(solution)/shard_map/ppermute | solution.py:370
  747.9 25.1 %copy-start.10 = (bf16[2,80,5120]{2,1,0:T(8,128)(2,1)}, bf16[2,80,5120]{2,1,0:T(8,128)(2,1)S(1)}, u32[]{:S(2)}) copy-start(bf16[2,80,5120]{2,1,0:T(8,128)(2,1)S(1)} %collective-permute-done.7.given) | copy-start | bytes 4915204
  747.9 79.8 %collective-permute-start.9 = (bf16[2,80,5120]{2,1,0:T(8,128)(2,1)}, bf16[2,80,5120]{2,1,0:T(8,128)(2,1)}, u32[]{:S(2)}, u32[]{:S(2)}) collective-permute-start(bf16[2,80,5120]{2,1,0:T(8,128)(2,1)} %collective-permute-done.8.came), channel_id=1, source_target_pairs={{0,1},{1,0},{2,3},{3,2},{4,5},{5,4},{6,7},{7,6},{8,9},{9,8},{10,11... | collective-permute-start | bytes 4915208 | tf_op jit(solution)/shard_map/ppermute | solution.py:370
  765.4 65.3 %collective-permute-start.14 = (bf16[2,320,1280]{2,1,0:T(8,128)(2,1)}, bf16[2,320,1280]{2,1,0:T(8,128)(2,1)}, u32[]{:S(2)}, u32[]{:S(2)}) collective-permute-start(bf16[2,320,1280]{2,1,0:T(8,128)(2,1)} %collective-permute-done.13.came), channel_id=1, source_target_pairs={{0,1},{1,0},{2,3},{3,2},{4,5},{5,4},{6,7},{7,6},{8,9},{9,8},{10,11... | collective-permute-start | bytes 4915208 | tf_op jit(solution)/shard_map/ppermute | solution.py:370
  806.3 1.2 copy-start.11
  806.3 1.7 copy-start.12
where the time goes:
time: 836 us; the launch traced here: 834 us
  Pallas kernels  714 us (85%)
  waiting for transfers between devices  93.6 us (11%)
  other arithmetic  15.1 us (2%)
    pallas_call x1, Pallas kernels, step_call(): pl.pallas_call(functools.partial(step_kernel, sizes), out_shape=[*arrays(...  655 us
    ppermute x15, waiting for transfers between devices, permute(): out.append(lax.ppermute(one, 'dp', pairs))  93.6 us
    pallas_call x6, Pallas kernels, local_call(): pl.pallas_call(functools.partial(kernel, block[0]), out_shape=jax.ShapeDt...  58.9 us
  transfers between devices with their start and end apart: 15, of which 6 were waited for; matrix products, arithmetic and copies ran while one was open for 2% of the time, Pallas kernels for 7%

commit v1 on v0

--- a/solution.py
+++ b/solution.py
@@ -31,15 +31,19 @@
     return lax.select(chip < 4, chip, 11 - chip)
 
 
-def each_tile(shape, body):
+STREAMS = ((0, (0, 1)), (1, (0, 1)), (2, (0,)), (2, (1,)))
+
+
+def each_tile(shape, body, first=0, count=None):
     rows, cols = shape
+    count = rows // ROWS if count is None else count
 
     def one(i, _):
         for c in range(cols // COLS):
             body(pl.ds(pl.multiple_of(i * ROWS, ROWS), ROWS), pl.ds(c * COLS, COLS))
         return 0
 
-    lax.fori_loop(0, rows // ROWS, one, 0)
+    lax.fori_loop(first, first + count, one, 0)
 
 
 def step_kernel(sizes, *refs):
@@ -52,9 +56,9 @@
         return taken
 
     terms, weights, old_m, old_v = take(n), take(n), take(n), take(n)
-    sums, edges, (factor_ref,), whole, lent, ring = take(n), take(n), take(1), take(n), take(n), take(n)
-    own, other, came, held, final, m_in, v_in = (take(n) for _ in range(7))
-    acc, totals, lend_s, lend_r, ring_s, ring_r, load_own, load_other, load_came, load_m, load_v, store, norm_s, norm_r = refs
+    sums, edges, (factor_ref,), whole, lent, ring = take(n), take(len(STREAMS)), take(1), take(n), take(n), take(n)
+    own, other, came, held, final, late, m_in, v_in = (take(n) for _ in range(8))
+    acc, totals, lend_s, lend_r, ring_s, ring_r, load_own, load_other, load_came, load_m, load_v, store, norm_s, norm_r, first_r = refs
 
     me = lax.axis_index("dp")
     core, chip = lax.rem(me, 2), lax.div(me, 2)
@@ -64,6 +68,8 @@
     following = ring_place(lax.rem(place + way + CHIPS, CHIPS)) * 2 + core
     jobs = [(k, layer) for k in range(n) for layer in range(2)]
     every = range(len(jobs))
+    edge_of = {(k, layer): edges[e].at[i] for e, (k, layers) in enumerate(STREAMS) for i, layer in enumerate(layers)}
+    pieces = [pl.ds(i * ROWS, ROWS) for i in range(sizes[0][0] // ROWS)]
 
     def rows_of(k, block):
         return pl.ds(pl.multiple_of(block * sizes[k][0], 16), sizes[k][0])
@@ -80,11 +86,19 @@
     def lend(step, j):
         k, layer = jobs[j]
         src = terms[k].at[layer, rows_of(k, block_at(step, 1 - core))]
-        return remote(src, lent[k].at[step, layer], lend_s.at[j], lend_r.at[step, j], partner)
+        dst = other[k].at[layer] if isinstance(step, int) and step == 0 else lent[k].at[step - 1, layer]
+        return remote(src, dst, lend_s.at[j], lend_r.at[step, j], partner)
+
+    def lend_piece(i):
+        return remote(came[0].at[0, pieces[i]], other[0].at[0, pieces[i]], lend_s.at[0], first_r.at[i], partner)
 
     def pass_on(step, j):
         k, layer = jobs[j]
-        return remote(held[k].at[layer], ring[k].at[step, layer], ring_s.at[j], ring_r.at[step, j], following)
+        dst = late[k].at[layer] if isinstance(step, int) and step == CHIPS - 2 else ring[k].at[step, layer]
+        return remote(held[k].at[layer], dst, ring_s.at[j], ring_r.at[step, j], following)
+
+    def pass_piece(i):
+        return remote(held[0].at[0, pieces[i]], ring[0].at[0, 0, pieces[i]], ring_s.at[0], ring_r.at[0, 0], following)
 
     def get_own(step, j):
         k, layer = jobs[j]
@@ -92,7 +106,7 @@
 
     def get_other(step, j):
         k, layer = jobs[j]
-        return pltpu.make_async_copy(lent[k].at[step, layer], other[k].at[layer], load_other.at[j])
+        return pltpu.make_async_copy(lent[k].at[step - 1, layer], other[k].at[layer], load_other.at[j])
 
     def get_came(step, j):
         k, layer = jobs[j]
@@ -120,30 +134,41 @@
         return 0
 
     lax.fori_loop(1, 16, greet, 0)
+    first_lent = pltpu.make_async_copy(terms[0].at[0, rows_of(0, block_at(0, 1 - core))], came[0].at[0], load_came.at[0])
+    first_lent.start()
     for j in every:
         get_own(0, j).start()
     acc[...] = jnp.zeros_like(acc)
+    first_lent.wait()
     pl.semaphore_wait(barrier, 15)
-    for j in every:
+    for i in range(len(pieces)):
+        lend_piece(i).start()
+    for j in every[1:]:
         lend(0, j).start()
 
     def one(step, j, first, last):
         k, layer = jobs[j]
-        a, b, c, h = (ref[k].at[layer] for ref in (own, other, came, final if last else held))
-        lend(step, j).wait_recv()
-        get_other(step, j).start()
+        a, b = own[k].at[layer], other[k].at[layer]
+        c, h = (late if last else came)[k].at[layer], (final if last else held)[k].at[layer]
+        cut = first and j == 0
+        if not cut:
+            lend(step, j).wait_recv()
         if not first:
+            get_other(step, j).start()
             pass_on(step - 1, j).wait_recv()
-            get_came(step - 1, j).start()
-        lend(step, j).wait_send()
-        if not last:
-            lend(step + 1, j).start()
+            if not last:
+                get_came(step - 1, j).start()
+        if not cut:
+            lend(step, j).wait_send()
+            if not last:
+                lend(step + 1, j).start()
         if not first:
             pass_on(step - 1, j).wait_send()
         get_own(step, j).wait()
-        get_other(step, j).wait()
         if not first:
-            get_came(step - 1, j).wait()
+            get_other(step, j).wait()
+            if not last:
+                get_came(step - 1, j).wait()
 
         def add(r, c_):
             so_far = a[r, c_].astype(F32) + b[r, c_].astype(F32)
@@ -155,9 +180,18 @@
                 g = rounded.astype(F32)
                 acc[...] += g * g
 
-        each_tile(sizes[k], add)
+        if cut:
+            for i in range(len(pieces)):
+                lend_piece(i).wait_recv()
+                each_tile(sizes[k], add, i, 1)
+                pass_piece(i).start()
+            lend(step, j).wait_send()
+            lend(step + 1, j).start()
+        else:
+            each_tile(sizes[k], add)
         if not last:
-            pass_on(step, j).start()
+            if not cut:
+                pass_on(step, j).start()
             get_own(step + 1, j).start()
         else:
             get_weight(j).start()
@@ -174,7 +208,9 @@
             one(step, j, False, False)
         return 0
 
-    lax.fori_loop(1, CHIPS - 1, middle, 0)
+    lax.fori_loop(1, CHIPS - 2, middle, 0)
+    for j in every:
+        one(CHIPS - 2, j, False, False)
     for j in every:
         one(CHIPS - 1, j, False, True)
 
@@ -212,8 +248,13 @@
 
     def hop(h, j, to_edge=False):
         k, layer = jobs[j]
-        dst = edges[k].at[layer] if to_edge else whole[k].at[layer, rows_at(k, h)]
+        dst = edge_of[jobs[j]] if to_edge else whole[k].at[layer, rows_at(k, h)]
         return remote(block_of(h, j), dst, ring_s.at[j], ring_r.at[h, j], following)
+
+    def hop_piece(i):
+        block = rows_at(0, 0)
+        dst = whole[0].at[0, pl.ds(pl.multiple_of(block.start + i * ROWS, ROWS), ROWS)]
+        return remote(held[0].at[0, pieces[i]], dst, ring_s.at[0], ring_r.at[0, 0], following)
 
     def give(h, j):
         k, layer = jobs[j]
@@ -230,8 +271,13 @@
         def update(r, c_):
             h[r, c_] = adamw(w[r, c_].astype(F32), m[r, c_], v[r, c_], a[r, c_].astype(F32) * factor)
 
-        each_tile(sizes[k], update)
-        hop(0, j).start()
+        if j == 0:
+            for i in range(len(pieces)):
+                each_tile(sizes[k], update, i, 1)
+                hop_piece(i).start()
+        else:
+            each_tile(sizes[k], update)
+            hop(0, j).start()
         give(0, j).start()
         keep(j).start()
 
@@ -270,16 +316,16 @@
         functools.partial(step_kernel, sizes),
         out_shape=[
             *arrays(()),
-            *arrays(()),
+            *(jax.ShapeDtypeStruct((len(layers), *sizes[k]), BF16) for k, layers in STREAMS),
             jax.ShapeDtypeStruct((8, 128), F32),
             *(jax.ShapeDtypeStruct(w.shape, BF16) for w in weights),
-            *arrays((CHIPS,)),
             *arrays((CHIPS - 1,)),
+            *arrays((CHIPS - 2,)),
         ],
         in_specs=[hbm] * (4 * n),
-        out_specs=[hbm] * (2 * n) + [vmem] + [hbm] * (3 * n),
+        out_specs=[hbm] * (n + len(STREAMS)) + [vmem] + [hbm] * (3 * n),
         scratch_shapes=[
-            *buffers(BF16) * 5,
+            *buffers(BF16) * 6,
             *buffers(F32) * 2,
             pltpu.VMEM((ROWS, COLS), F32),
             pltpu.VMEM((16, 8, 128), F32),
@@ -290,12 +336,14 @@
             *[dma((jobs,))] * 6,
             dma((16,)),
             dma((16,)),
+            dma((sizes[0][0] // ROWS,)),
         ],
         compiler_params=pltpu.CompilerParams(collective_id=0, has_side_effects=True, vmem_limit_bytes=VMEM_LIMIT),
         cost_estimate=pl.CostEstimate(flops=400_000_000, bytes_accessed=300_000_000, transcendentals=0),
         name="step_kernel",
     )(*terms, *weights, *m, *v)
-    return out[:n], out[n : 2 * n], out[2 * n][0, 0], out[2 * n + 1 : 3 * n + 1]
+    cut = n + len(STREAMS)
+    return out[:n], out[n:cut], out[cut][0, 0], out[cut + 1 : cut + 1 + n]
 
 
 def move(tasks, slots, load, store):
@@ -326,42 +374,64 @@
     return pl.ds(pl.multiple_of(block * rows, 16), rows)
 
 
-def fill_kernel(rows, whole, edge, edge_given, came, given, out, slots, load, store):
+def fill_kernel(k, rows, whole, *refs):
+    *streams, out, slots, load, store = refs
     tasks = []
     for layer in range(2):
         for mine in (True, False):
             for h in range(HOPS):
-                at = out.at[layer, rows_back(h, rows, mine)]
-                tasks.append((whole.at[layer, rows_back(h, rows, mine)], at))
-        for h, mine, src in ((HOPS, True, edge), (HOPS, False, edge_given), (HOPS + 1, True, came), (HOPS + 1, False, given)):
-            tasks.append((src.at[layer], out.at[layer, rows_back(h, rows, mine)]))
+                at = rows_back(h, rows, mine)
+                tasks.append((whole.at[layer, at], out.at[layer, at]))
+    for i, layers in enumerate(layers for of, layers in STREAMS if of == k):
+        for h, mine, src in zip((HOPS, HOPS, HOPS + 1, HOPS + 1), (True, False) * 2, streams[4 * i : 4 * i + 4], strict=True):
+            for at, layer in enumerate(layers):
+                tasks.append((src.at[at], out.at[layer, rows_back(h, rows, mine)]))
     move(tasks, slots, load, store)
 
 
-def finish_kernel(rows, _, came, given, out, slots, load, store):
-    tasks = []
-    for layer in range(2):
-        for mine, src in ((True, came), (False, given)):
-            tasks.append((src.at[layer], out.at[layer, rows_back(HOPS + 2, rows, mine)]))
-    move(tasks, slots, load, store)
-
-
-def local_call(kernel, arrays, block, aliases, flops):
+def fill(k, rows, whole, streams):
     hbm = pl.BlockSpec(memory_space=pltpu.HBM)
     return pl.pallas_call(
-        functools.partial(kernel, block[0]),
-        out_shape=jax.ShapeDtypeStruct(arrays[0].shape, BF16),
-        in_specs=[hbm] * len(arrays),
+        functools.partial(fill_kernel, k, rows),
+        out_shape=jax.ShapeDtypeStruct(whole.shape, BF16),
+        in_specs=[hbm] * (1 + len(streams)),
         out_specs=hbm,
-        input_output_aliases=aliases,
         scratch_shapes=[
-            pltpu.VMEM((SLOTS, *block), BF16),
+            pltpu.VMEM((SLOTS, rows, whole.shape[2]), BF16),
             pltpu.SemaphoreType.DMA((SLOTS,)),
             pltpu.SemaphoreType.DMA((SLOTS,)),
         ],
         compiler_params=pltpu.CompilerParams(vmem_limit_bytes=VMEM_LIMIT),
-        cost_estimate=pl.CostEstimate(flops=flops, bytes_accessed=arrays[0].size * 4, transcendentals=0),
-    )(*arrays)
+        cost_estimate=pl.CostEstimate(flops=60_000_000, bytes_accessed=whole.size * 4, transcendentals=0),
+        name="fill",
+    )(whole, *streams)
+
+
+def finish_kernel(layers, rows, _, came, given, out, store):
+    copies = []
+    for at, layer in enumerate(layers):
+        for mine, src in ((True, came), (False, given)):
+            dst = out.at[layer, rows_back(HOPS + 2, rows, mine)]
+            copies.append(pltpu.make_async_copy(src.at[at], dst, store.at[len(copies)]))
+    for copy in copies:
+        copy.start()
+    for copy in copies:
+        copy.wait()
+
+
+def finish(layers, rows, w, came, given):
+    hbm, vmem = pl.BlockSpec(memory_space=pltpu.HBM), pl.BlockSpec(memory_space=pltpu.VMEM)
+    return pl.pallas_call(
+        functools.partial(finish_kernel, layers, rows),
+        out_shape=jax.ShapeDtypeStruct(w.shape, BF16),
+        in_specs=[hbm, vmem, vmem],
+        out_specs=hbm,
+        input_output_aliases={0: 0},
+        scratch_shapes=[pltpu.SemaphoreType.DMA((2 * len(layers),))],
+        compiler_params=pltpu.CompilerParams(vmem_limit_bytes=8 << 20),
+        cost_estimate=pl.CostEstimate(flops=8_000_000, bytes_accessed=came.size * 8, transcendentals=0),
+        name="finish",
+    )(w, came, given)
 
 
 def permute(arrays, pairs):
@@ -384,11 +454,13 @@
         edge_given, given = permute(edges, across), permute(came, across)
         last_given = permute(last, across)
         new = [moments(a, b, g.astype(F32) * factor) for a, b, g in zip(m, v, sums, strict=True)]
-        whole = []
+        whole = list(gathered)
         for k, one in enumerate(m):
-            block = one.shape[1:]
-            w = local_call(fill_kernel, (gathered[k], edges[k], edge_given[k], came[k], given[k]), block, {}, 60_000_000)
-            whole.append(local_call(finish_kernel, (w, last[k], last_given[k]), block, {0: 0}, 8_000_000))
+            mine = [e for e, (of, _) in enumerate(STREAMS) if of == k]
+            streams = [part[e] for e in mine for part in (edges, edge_given, came, given)]
+            whole[k] = fill(k, one.shape[1], whole[k], streams)
+        for e, (k, layers) in enumerate(STREAMS):
+            whole[k] = finish(layers, m[k].shape[1], whole[k], last[e], last_given[e])
         return (*whole, *(one[0] for one in new), *(one[1] for one in new))
 
     all_of, cut = P(None, None, None), P(None, "dp", None)

time: 836 us -> 831 us (level)
    ppermute x15 -> x20, waiting for transfers between devices: 93.6 us -> 87.8 us  [permute(): out.append(lax.ppermute(one, 'dp', pairs))]
    pallas_call x6 -> x7, Pallas kernels: 58.9 us -> 58.7 us  [the longest x3 50 us: fill(): pl.pallas_call(functools.partial(fill_kernel, k, rows), out_shape=jax.Sha...]
  transfers between devices with their start and end apart: 15 -> 20, of which waited for: 6 -> 6; matrix products, arithmetic and copies ran while one was open for 2% -> 2% of each run, Pallas kernels for 7% -> 7%
where the time goes in v1:
time: 831 us; the launch traced here: 829 us
  Pallas kernels  710 us (85%)
  waiting for transfers between devices  87.8 us (11%)
  other arithmetic  16.2 us (2%)
  starting transfers between devices  10.7 us (1%)
    pallas_call x1, Pallas kernels, step_call(): pl.pallas_call(functools.partial(step_kernel, sizes), out_shape=[*arrays(...  651 us
    ppermute x20, waiting for transfers between devices, permute(): out.append(lax.ppermute(one, 'dp', pairs))  87.8 us
    pallas_call x3, Pallas kernels, fill(): pl.pallas_call(functools.partial(fill_kernel, k, rows), out_shape=jax.Sha...  50 us
  transfers between devices with their start and end apart: 20, of which 6 were waited for; matrix products, arithmetic and copies ran while one was open for 2% of the time, Pallas kernels for 7%

profile of v1, /device:TPU:0, one launch (start us, length us, event | category | flops | bytes accessed | tf_op | source)
XLA Modules:
  0.0 829.2 jit_solution(7856974364888468357)
XLA Ops:
  0.6 651.3 %step_kernel.1 = (bf16[2,80,5120]{2,1,0:T(8,128)(2,1)}, bf16[2,80,5120]{2,1,0:T(8,128)(2,1)}, bf16[2,320,1280]{2,1,0:T(8,128)(2,1)}, bf16[2,80,5120]{2,1,0:T(8,1...) custom-call(bf16[2,1280,5120]{2,1,0:T(8,128)(2,1)} %bitcast.4, ...), custom_call_target="tpu_custom_call" | custom-call | flops 400000000 | bytes 300000000 | tf_op jit(solution)/shard_map/step_kernel/pallas_call | solution.py:315
  652.0 1.2 collective-permute-start.11
  653.2 0.0 collective-permute-start.10
  653.2 0.8 collective-permute-start.14
  654.0 0.7 collective-permute-start.1
  654.7 1.5 collective-permute-start.6
  656.2 8.4 %collective-permute-done.11.refs_2_ = bf16[1,320,1280]{2,1,0:T(8,128)(2,1)S(1)} collective-permute-done((bf16[1,320,1280]{2,1,0:T(8,128)(2,1)}, bf16[1,320,1280]{2,1,0:T(8,128)(2,1)S(1)}, u32[]{:S(2)}, u32[]{:S(2)}) %collective-permute-start.11) | collective-permute-done | bytes 819232 | tf_op jit(solution)/shard_map/ppermute | solution.py:440
  664.6 0.0 copy-start.13
  664.6 1.2 collective-permute-start.16
  665.8 7.6 collective-permute-done.14.refs_6_
  673.4 0.0 collective-permute-done.13.refs_5_
  673.4 1.2 collective-permute-start.18
  674.6 42.7 %collective-permute-done.16.came = bf16[1,320,1280]{2,1,0:T(8,128)(2,1)S(1)} collective-permute-done((bf16[1,320,1280]{2,1,0:T(8,128)(2,1)S(1)}, bf16[1,320,1280]{2,1,0:T(8,128)(2,1)S(1)}, u32[]{:S(2)}, u32[]{:S(2)}) %collective-permute-start.16) | collective-permute-done | bytes 819232 | tf_op jit(solution)/shard_map/ppermute | solution.py:440
  717.3 0.0 collective-permute-start.15
  717.3 0.5 collective-permute-start
  717.8 0.0 collective-permute-done.1.refs_2_
  717.8 1.2 collective-permute-start.3
  719.0 0.0 collective-permute-done.6.refs_2_
  719.0 0.9 collective-permute-start.8
  719.9 1.2 slice.3
  721.1 5.0 collective-permute-done.18.came
  726.0 0.0 collective-permute-start.17
  726.1 0.5 collective-permute-start.19
  726.6 0.4 copy-done.17
  727.0 8.9 %fusion.2 = (f32[2,320,1280]{2,1,0:T(8,128)}, f32[2,320,1280]{2,1,0:T(8,128)}) fusion(f32[2,320,1280]{2,1,0:T(8,128)} %refs_11_.1, bf16[2,320,1280]{2,1,0:T(8,128)(2,1)} %get-tuple-element.30, f32[]{:T(128)} %bitcast.3, f32[2,320,1280]{2,1,0:T(8,128)} %refs_8_.1), kind=kLoop, calls=%fused_computation.5 | loop fusion | flops 7372800 | bytes 14745604 | tf_op jit(solution)/shard_map/add | solution.py:21
  735.9 0.0 collective-permute-done.refs_1_
  735.9 0.0 copy-start.10
  735.9 0.5 collective-permute-start.5
  736.5 0.1 collective-permute-start.2
  736.6 0.4 collective-permute-start.7
  737.0 6.6 collective-permute-done.3.came
  743.6 17.6 %collective-permute-done.8.came = bf16[2,80,5120]{2,1,0:T(8,128)(2,1)S(1)} collective-permute-done((bf16[2,80,5120]{2,1,0:T(8,128)(2,1)}, bf16[2,80,5120]{2,1,0:T(8,128)(2,1)S(1)}, u32[]{:S(2)}, u32[]{:S(2)}) %collective-permute-start.8) | collective-permute-done | bytes 1638432 | tf_op jit(solution)/shard_map/ppermute | solution.py:440
  761.2 0.0 collective-permute-start.9
  761.2 7.3 fusion
  768.5 16.7 %fill.5._ = bf16[2,5120,1280]{2,1,0:T(8,128)(2,1)} custom-call(bf16[2,5120,1280]{2,1,0:T(8,128)(2,1)} %get-tuple-element.24.whole, bf16[1,320,1280]{2,1,0:T(8,128)(2,1)} %get-tuple-element.25.refs_0_, bf16[1,320,1280]{2,1,0:T(8,128)(2,1)} %copy-done.13, bf16[1,320,1280]{2,1,0:T(8,128)(2,1)} %copy-done.12, bf16[1,320,1280]{2,1,0:T(8,128)(2,1)} %copy-done.16, ...), custom_call_target="tpu_custom_call" | custom-call | flops 60000000 | bytes 52428800 | tf_op jit(solution)/shard_map/fill/pallas_call | solution.py:394
  785.2 1.1 copy-done.3
  786.3 1.2 finish.6._
  787.5 0.5 copy-done.1
  788.0 0.3 copy-done.5
  788.3 1.2 finish.7
  789.5 0.0 collective-permute-done.2.refs_3_
  789.5 16.7 %fill.3._ = bf16[2,1280,5120]{2,1,0:T(8,128)(2,1)} custom-call(bf16[2,1280,5120]{2,1,0:T(8,128)(2,1)} %get-tuple-element.20.whole, bf16[2,80,5120]{2,1,0:T(8,128)(2,1)} %get-tuple-element.21.refs_0_, bf16[2,80,5120]{2,1,0:T(8,128)(2,1)} %copy-done.10, bf16[2,80,5120]{2,1,0:T(8,128)(2,1)} %collective-permute-done.1.refs_2_, ...), custom_call_target="tpu_custom_call" | custom-call | flops 60000000 | bytes 52428800 | tf_op jit(solution)/shard_map/fill/pallas_call | solution.py:394
  806.2 0.0 collective-permute-done.5.refs_1_
  806.2 0.0 collective-permute-done.7.refs_3_
  806.2 16.7 %fill.4._ = bf16[2,1280,5120]{2,1,0:T(8,128)(2,1)} custom-call(bf16[2,1280,5120]{2,1,0:T(8,128)(2,1)} %get-tuple-element.22.whole, bf16[2,80,5120]{2,1,0:T(8,128)(2,1)} %get-tuple-element.23.refs_0_, bf16[2,80,5120]{2,1,0:T(8,128)(2,1)} %collective-permute-done.5.refs_1_, bf16[2,80,5120]{2,1,0:T(8,128)(2,1)} %collective-permute-done.6.refs_2_, ...), custom_call_target="tpu_custom_call" | custom-call | flops 60000000 | bytes 52428800 | tf_op jit(solution)/shard_map/fill/pallas_call | solution.py:394
  822.9 3.2 finish.4
  826.1 0.0 collective-permute-done.9.given
  826.1 3.2 finish.5
  (39 shorter events, 0.1 us)
Async XLA Ops:
  652.0 12.6 %collective-permute-start.11 = (bf16[1,320,1280]{2,1,0:T(8,128)(2,1)}, bf16[1,320,1280]{2,1,0:T(8,128)(2,1)S(1)}, u32[]{:S(2)}, u32[]{:S(2)}) collective-permute-start(bf16[1,320,1280]{2,1,0:T(8,128)(2,1)} %get-tuple-element.25.refs_0_), channel_id=1, source_target_pairs={{0,2},{1,9},{2,4},{3,1},{4,6},{5,3},{6,14},{7,5},{8,0},{9,11},{10,... | collective-permute-start | bytes 2457608 | tf_op jit(solution)/shard_map/ppermute | solution.py:440
  653.2 11.4 %collective-permute-start.10 = (bf16[1,320,1280]{2,1,0:T(8,128)(2,1)}, bf16[1,320,1280]{2,1,0:T(8,128)(2,1)S(1)}, u32[]{:S(2)}, u32[]{:S(2)}) collective-permute-start(bf16[1,320,1280]{2,1,0:T(8,128)(2,1)} %get-tuple-element.25.refs_0_), channel_id=1, source_target_pairs={{0,1},{1,0},{2,3},{3,2},{4,5},{5,4},{6,7},{7,6},{8,9},{9,8},{10,11... | collective-permute-start | bytes 2457608 | tf_op jit(solution)/shard_map/ppermute | solution.py:440
  653.2 20.2 %collective-permute-start.14 = (bf16[1,320,1280]{2,1,0:T(8,128)(2,1)}, bf16[1,320,1280]{2,1,0:T(8,128)(2,1)S(1)}, u32[]{:S(2)}, u32[]{:S(2)}) collective-permute-start(bf16[1,320,1280]{2,1,0:T(8,128)(2,1)} %get-tuple-element.26.refs_4_), channel_id=1, source_target_pairs={{0,2},{1,9},{2,4},{3,1},{4,6},{5,3},{6,14},{7,5},{8,0},{9,11},{10,... | collective-permute-start | bytes 2457608 | tf_op jit(solution)/shard_map/ppermute | solution.py:440
  654.0 63.8 %collective-permute-start.1 = (bf16[2,80,5120]{2,1,0:T(8,128)(2,1)}, bf16[2,80,5120]{2,1,0:T(8,128)(2,1)}, u32[]{:S(2)}, u32[]{:S(2)}) collective-permute-start(bf16[2,80,5120]{2,1,0:T(8,128)(2,1)} %get-tuple-element.21.refs_0_), channel_id=1, source_target_pairs={{0,2},{1,9},{2,4},{3,1},{4,6},{5,3},{6,14},{7,5},{8,0},{9,11},{10,... | collective-permute-start | bytes 4915208 | tf_op jit(solution)/shard_map/ppermute | solution.py:440
  654.7 64.3 %collective-permute-start.6 = (bf16[2,80,5120]{2,1,0:T(8,128)(2,1)}, bf16[2,80,5120]{2,1,0:T(8,128)(2,1)}, u32[]{:S(2)}, u32[]{:S(2)}) collective-permute-start(bf16[2,80,5120]{2,1,0:T(8,128)(2,1)} %get-tuple-element.23.refs_0_), channel_id=1, source_target_pairs={{0,2},{1,9},{2,4},{3,1},{4,6},{5,3},{6,14},{7,5},{8,0},{9,11},{10,... | collective-permute-start | bytes 4915208 | tf_op jit(solution)/shard_map/ppermute | solution.py:440
  664.6 53.2 %copy-start.12 = (bf16[1,320,1280]{2,1,0:T(8,128)(2,1)}, bf16[1,320,1280]{2,1,0:T(8,128)(2,1)S(1)}, u32[]{:S(2)}) copy-start(bf16[1,320,1280]{2,1,0:T(8,128)(2,1)S(1)} %collective-permute-done.11.refs_2_) | copy-start | bytes 2457604
  664.6 8.8 %collective-permute-start.13 = (bf16[1,320,1280]{2,1,0:T(8,128)(2,1)}, bf16[1,320,1280]{2,1,0:T(8,128)(2,1)S(1)}, u32[]{:S(2)}, u32[]{:S(2)}) collective-permute-start(bf16[1,320,1280]{2,1,0:T(8,128)(2,1)} %get-tuple-element.26.refs_4_), channel_id=1, source_target_pairs={{0,1},{1,0},{2,3},{3,2},{4,5},{5,4},{6,7},{7,6},{8,9},{9,8},{10,11... | collective-permute-start | bytes 2457608 | tf_op jit(solution)/shard_map/ppermute | solution.py:440
  664.6 53.2 %copy-start.13 = (bf16[1,320,1280]{2,1,0:T(8,128)(2,1)}, bf16[1,320,1280]{2,1,0:T(8,128)(2,1)S(1)}, u32[]{:S(2)}) copy-start(bf16[1,320,1280]{2,1,0:T(8,128)(2,1)S(1)} %collective-permute-done.10.refs_1_) | copy-start | bytes 2457604
  664.6 52.6 %collective-permute-start.16 = (bf16[1,320,1280]{2,1,0:T(8,128)(2,1)S(1)}, bf16[1,320,1280]{2,1,0:T(8,128)(2,1)S(1)}, u32[]{:S(2)}, u32[]{:S(2)}) collective-permute-start(bf16[1,320,1280]{2,1,0:T(8,128)(2,1)S(1)} %collective-permute-done.11.refs_2_), channel_id=1, source_target_pairs={{0,2},{1,9},{2,4},{3,1},{4,6},{5,3},{6,14},{7,5},{8,0},{9,11},{10,... | collective-permute-start | bytes 2457608 | tf_op jit(solution)/shard_map/ppermute | solution.py:440
  673.4 53.2 %copy-start.14 = (bf16[1,320,1280]{2,1,0:T(8,128)(2,1)}, bf16[1,320,1280]{2,1,0:T(8,128)(2,1)S(1)}, u32[]{:S(2)}) copy-start(bf16[1,320,1280]{2,1,0:T(8,128)(2,1)S(1)} %collective-permute-done.14.refs_6_) | copy-start | bytes 2457604
  673.4 43.9 %collective-permute-start.12 = (bf16[1,320,1280]{2,1,0:T(8,128)(2,1)S(1)}, bf16[1,320,1280]{2,1,0:T(8,128)(2,1)S(1)}, u32[]{:S(2)}, u32[]{:S(2)}) collective-permute-start(bf16[1,320,1280]{2,1,0:T(8,128)(2,1)S(1)} %collective-permute-done.11.refs_2_), channel_id=1, source_target_pairs={{0,1},{1,0},{2,3},{3,2},{4,5},{5,4},{6,7},{7,6},{8,9},{9,8},{10,11... | collective-permute-start | bytes 2457608 | tf_op jit(solution)/shard_map/ppermute | solution.py:440
  673.4 45.6 %copy-start.15 = (bf16[1,320,1280]{2,1,0:T(8,128)(2,1)}, bf16[1,320,1280]{2,1,0:T(8,128)(2,1)S(1)}, u32[]{:S(2)}) copy-start(bf16[1,320,1280]{2,1,0:T(8,128)(2,1)S(1)} %collective-permute-done.13.refs_5_) | copy-start | bytes 2457604
  673.4 52.6 %collective-permute-start.18 = (bf16[1,320,1280]{2,1,0:T(8,128)(2,1)S(1)}, bf16[1,320,1280]{2,1,0:T(8,128)(2,1)S(1)}, u32[]{:S(2)}, u32[]{:S(2)}) collective-permute-start(bf16[1,320,1280]{2,1,0:T(8,128)(2,1)S(1)} %collective-permute-done.14.refs_6_), channel_id=1, source_target_pairs={{0,2},{1,9},{2,4},{3,1},{4,6},{5,3},{6,14},{7,5},{8,0},{9,11},{10,... | collective-permute-start | bytes 2457608 | tf_op jit(solution)/shard_map/ppermute | solution.py:440
  717.3 8.8 %collective-permute-start.15 = (bf16[1,320,1280]{2,1,0:T(8,128)(2,1)S(1)}, bf16[1,320,1280]{2,1,0:T(8,128)(2,1)S(1)}, u32[]{:S(2)}, u32[]{:S(2)}) collective-permute-start(bf16[1,320,1280]{2,1,0:T(8,128)(2,1)S(1)} %collective-permute-done.14.refs_6_), channel_id=1, source_target_pairs={{0,1},{1,0},{2,3},{3,2},{4,5},{5,4},{6,7},{7,6},{8,9},{9,8},{10,11... | collective-permute-start | bytes 2457608 | tf_op jit(solution)/shard_map/ppermute | solution.py:440
  717.3 1.7 copy-start.16
  717.3 18.6 %collective-permute-start = (bf16[2,80,5120]{2,1,0:T(8,128)(2,1)}, bf16[2,80,5120]{2,1,0:T(8,128)(2,1)S(1)}, u32[]{:S(2)}, u32[]{:S(2)}) collective-permute-start(bf16[2,80,5120]{2,1,0:T(8,128)(2,1)} %get-tuple-element.21.refs_0_), channel_id=1, source_target_pairs={{0,1},{1,0},{2,3},{3,2},{4,5},{5,4},{6,7},{7,6},{8,9},{9,8},{10,11... | collective-permute-start | bytes 4915208 | tf_op jit(solution)/shard_map/ppermute | solution.py:440
  717.8 25.8 %collective-permute-start.3 = (bf16[2,80,5120]{2,1,0:T(8,128)(2,1)}, bf16[2,80,5120]{2,1,0:T(8,128)(2,1)S(1)}, u32[]{:S(2)}, u32[]{:S(2)}) collective-permute-start(bf16[2,80,5120]{2,1,0:T(8,128)(2,1)} %collective-permute-done.1.refs_2_), channel_id=1, source_target_pairs={{0,2},{1,9},{2,4},{3,1},{4,6},{5,3},{6,14},{7,5},{8,0},{9,11},{10,... | collective-permute-start | bytes 4915208 | tf_op jit(solution)/shard_map/ppermute | solution.py:440
  719.0 42.2 %collective-permute-start.8 = (bf16[2,80,5120]{2,1,0:T(8,128)(2,1)}, bf16[2,80,5120]{2,1,0:T(8,128)(2,1)S(1)}, u32[]{:S(2)}, u32[]{:S(2)}) collective-permute-start(bf16[2,80,5120]{2,1,0:T(8,128)(2,1)} %collective-permute-done.6.refs_2_), channel_id=1, source_target_pairs={{0,2},{1,9},{2,4},{3,1},{4,6},{5,3},{6,14},{7,5},{8,0},{9,11},{10,... | collective-permute-start | bytes 4915208 | tf_op jit(solution)/shard_map/ppermute | solution.py:440
  726.0 9.9 %copy-start = (bf16[1,320,1280]{2,1,0:T(8,128)(2,1)}, bf16[1,320,1280]{2,1,0:T(8,128)(2,1)S(1)}, u32[]{:S(2)}) copy-start(bf16[1,320,1280]{2,1,0:T(8,128)(2,1)S(1)} %collective-permute-done.18.came) | copy-start | bytes 2457604
  726.0 10.4 %collective-permute-start.17 = (bf16[1,320,1280]{2,1,0:T(8,128)(2,1)S(1)}, bf16[1,320,1280]{2,1,0:T(8,128)(2,1)S(1)}, u32[]{:S(2)}, u32[]{:S(2)}) collective-permute-start(bf16[1,320,1280]{2,1,0:T(8,128)(2,1)S(1)} %collective-permute-done.16.came), channel_id=1, source_target_pairs={{0,1},{1,0},{2,3},{3,2},{4,5},{5,4},{6,7},{7,6},{8,9},{9,8},{10,11... | collective-permute-start | bytes 2457608 | tf_op jit(solution)/shard_map/ppermute | solution.py:440
  726.1 1.0 copy-start.17
  726.1 10.5 %collective-permute-start.19 = (bf16[1,320,1280]{2,1,0:T(8,128)(2,1)S(1)}, bf16[1,320,1280]{2,1,0:T(8,128)(2,1)S(1)}, u32[]{:S(2)}, u32[]{:S(2)}) collective-permute-start(bf16[1,320,1280]{2,1,0:T(8,128)(2,1)S(1)} %collective-permute-done.18.came), channel_id=1, source_target_pairs={{0,1},{1,0},{2,3},{3,2},{4,5},{5,4},{6,7},{7,6},{8,9},{9,8},{10,11... | collective-permute-start | bytes 2457608 | tf_op jit(solution)/shard_map/ppermute | solution.py:440
  727.0 34.2 %copy-start.6 = (f32[2,80,5120]{2,1,0:T(8,128)S(1)}, f32[2,80,5120]{2,1,0:T(8,128)}, u32[]{:S(2)}) copy-start(f32[2,80,5120]{2,1,0:T(8,128)} %refs_6_.1) | copy-start | bytes 9830404
  727.0 34.2 %copy-start.7 = (f32[2,80,5120]{2,1,0:T(8,128)S(1)}, f32[2,80,5120]{2,1,0:T(8,128)}, u32[]{:S(2)}) copy-start(f32[2,80,5120]{2,1,0:T(8,128)} %refs_7_.1) | copy-start | bytes 9830404
  727.0 34.2 %copy-start.8 = (f32[2,80,5120]{2,1,0:T(8,128)S(1)}, f32[2,80,5120]{2,1,0:T(8,128)}, u32[]{:S(2)}) copy-start(f32[2,80,5120]{2,1,0:T(8,128)} %refs_9_.1) | copy-start | bytes 9830404
  727.0 34.2 %copy-start.9 = (f32[2,80,5120]{2,1,0:T(8,128)S(1)}, f32[2,80,5120]{2,1,0:T(8,128)}, u32[]{:S(2)}) copy-start(f32[2,80,5120]{2,1,0:T(8,128)} %refs_10_.1) | copy-start | bytes 9830404
  727.0 34.2 %copy-start.11 = (bf16[2,80,5120]{2,1,0:T(8,128)(2,1)S(1)}, bf16[2,80,5120]{2,1,0:T(8,128)(2,1)}, u32[]{:S(2)}) copy-start(bf16[2,80,5120]{2,1,0:T(8,128)(2,1)} %get-tuple-element.27) | copy-start | bytes 4915204
  735.9 32.6 %copy-start.10 = (bf16[2,80,5120]{2,1,0:T(8,128)(2,1)}, bf16[2,80,5120]{2,1,0:T(8,128)(2,1)S(1)}, u32[]{:S(2)}) copy-start(bf16[2,80,5120]{2,1,0:T(8,128)(2,1)S(1)} %collective-permute-done.refs_1_) | copy-start | bytes 4915204
  735.9 70.2 %collective-permute-start.5 = (bf16[2,80,5120]{2,1,0:T(8,128)(2,1)}, bf16[2,80,5120]{2,1,0:T(8,128)(2,1)}, u32[]{:S(2)}, u32[]{:S(2)}) collective-permute-start(bf16[2,80,5120]{2,1,0:T(8,128)(2,1)} %get-tuple-element.23.refs_0_), channel_id=1, source_target_pairs={{0,1},{1,0},{2,3},{3,2},{4,5},{5,4},{6,7},{7,6},{8,9},{9,8},{10,11... | collective-permute-start | bytes 4915208 | tf_op jit(solution)/shard_map/ppermute | solution.py:440
  736.5 32.0 %copy-start.2 = (bf16[1,320,1280]{2,1,0:T(8,128)(2,1)}, bf16[1,320,1280]{2,1,0:T(8,128)(2,1)S(1)}, u32[]{:S(2)}) copy-start(bf16[1,320,1280]{2,1,0:T(8,128)(2,1)S(1)} %collective-permute-done.17.given) | copy-start | bytes 2457604
  736.5 53.0 %collective-permute-start.2 = (bf16[2,80,5120]{2,1,0:T(8,128)(2,1)}, bf16[2,80,5120]{2,1,0:T(8,128)(2,1)}, u32[]{:S(2)}, u32[]{:S(2)}) collective-permute-start(bf16[2,80,5120]{2,1,0:T(8,128)(2,1)} %collective-permute-done.1.refs_2_), channel_id=1, source_target_pairs={{0,1},{1,0},{2,3},{3,2},{4,5},{5,4},{6,7},{7,6},{8,9},{9,8},{10,11... | collective-permute-start | bytes 4915208 | tf_op jit(solution)/shard_map/ppermute | solution.py:440
  736.6 31.9 %copy-start.4 = (bf16[1,320,1280]{2,1,0:T(8,128)(2,1)}, bf16[1,320,1280]{2,1,0:T(8,128)(2,1)S(1)}, u32[]{:S(2)}) copy-start(bf16[1,320,1280]{2,1,0:T(8,128)(2,1)S(1)} %collective-permute-done.19.given) | copy-start | bytes 2457604
  736.6 69.6 %collective-permute-start.7 = (bf16[2,80,5120]{2,1,0:T(8,128)(2,1)}, bf16[2,80,5120]{2,1,0:T(8,128)(2,1)}, u32[]{:S(2)}, u32[]{:S(2)}) collective-permute-start(bf16[2,80,5120]{2,1,0:T(8,128)(2,1)} %collective-permute-done.6.refs_2_), channel_id=1, source_target_pairs={{0,1},{1,0},{2,3},{3,2},{4,5},{5,4},{6,7},{7,6},{8,9},{9,8},{10,11... | collective-permute-start | bytes 4915208 | tf_op jit(solution)/shard_map/ppermute | solution.py:440
  743.6 79.3 %collective-permute-start.4 = (bf16[2,80,5120]{2,1,0:T(8,128)(2,1)S(1)}, bf16[2,80,5120]{2,1,0:T(8,128)(2,1)}, u32[]{:S(2)}, u32[]{:S(2)}) collective-permute-start(bf16[2,80,5120]{2,1,0:T(8,128)(2,1)S(1)} %collective-permute-done.3.came), channel_id=1, source_target_pairs={{0,1},{1,0},{2,3},{3,2},{4,5},{5,4},{6,7},{7,6},{8,9},{9,8},{10,11... | collective-permute-start | bytes 4915208 | tf_op jit(solution)/shard_map/ppermute | solution.py:440
  761.2 64.9 %collective-permute-start.9 = (bf16[2,80,5120]{2,1,0:T(8,128)(2,1)S(1)}, bf16[2,80,5120]{2,1,0:T(8,128)(2,1)}, u32[]{:S(2)}, u32[]{:S(2)}) collective-permute-start(bf16[2,80,5120]{2,1,0:T(8,128)(2,1)S(1)} %collective-permute-done.8.came), channel_id=1, source_target_pairs={{0,1},{1,0},{2,3},{3,2},{4,5},{5,4},{6,7},{7,6},{8,9},{9,8},{10,11... | collective-permute-start | bytes 4915208 | tf_op jit(solution)/shard_map/ppermute | solution.py:440
  785.2 1.1 copy-start.3
  786.3 1.7 copy-start.1
  786.3 2.0 copy-start.5

commit v2 on v1

--- a/solution.py
+++ b/solution.py
@@ -12,6 +12,7 @@
 CHIPS = 8
 HOPS = 5
 VMEM_LIMIT = 60 * 1024 * 1024
+ENDS = 4
 SLOTS, LAG = 8, 4
 ROWS = 16
 COLS = 1280
@@ -58,7 +59,7 @@
     terms, weights, old_m, old_v = take(n), take(n), take(n), take(n)
     sums, edges, (factor_ref,), whole, lent, ring = take(n), take(len(STREAMS)), take(1), take(n), take(n), take(n)
     own, other, came, held, final, late, m_in, v_in = (take(n) for _ in range(8))
-    acc, totals, lend_s, lend_r, ring_s, ring_r, load_own, load_other, load_came, load_m, load_v, store, norm_s, norm_r, first_r = refs
+    acc, totals, lend_s, lend_r, ring_s, ring_r, load_own, load_other, load_came, load_m, load_v, store, norm_s, norm_r, first_r, late_r = refs
 
     me = lax.axis_index("dp")
     core, chip = lax.rem(me, 2), lax.div(me, 2)
@@ -70,6 +71,8 @@
     every = range(len(jobs))
     edge_of = {(k, layer): edges[e].at[i] for e, (k, layers) in enumerate(STREAMS) for i, layer in enumerate(layers)}
     pieces = [pl.ds(i * ROWS, ROWS) for i in range(sizes[0][0] // ROWS)]
+    end = len(jobs) - 1
+    quarter = sizes[-1][0] // ENDS
 
     def rows_of(k, block):
         return pl.ds(pl.multiple_of(block * sizes[k][0], 16), sizes[k][0])
@@ -99,6 +102,10 @@
 
     def pass_piece(i):
         return remote(held[0].at[0, pieces[i]], ring[0].at[0, 0, pieces[i]], ring_s.at[0], ring_r.at[0, 0], following)
+
+    def end_piece(i):
+        rows = pl.ds(i * quarter, quarter)
+        return remote(held[-1].at[1, rows], late[-1].at[1, rows], ring_s.at[end], late_r.at[i], following)
 
     def get_own(step, j):
         k, layer = jobs[j]
@@ -151,11 +158,13 @@
         a, b = own[k].at[layer], other[k].at[layer]
         c, h = (late if last else came)[k].at[layer], (final if last else held)[k].at[layer]
         cut = first and j == 0
+        ending = j == end and isinstance(step, int) and step >= CHIPS - 2
         if not cut:
             lend(step, j).wait_recv()
         if not first:
             get_other(step, j).start()
-            pass_on(step - 1, j).wait_recv()
+            if not (last and j == end):
+                pass_on(step - 1, j).wait_recv()
             if not last:
                 get_came(step - 1, j).start()
         if not cut:
@@ -187,10 +196,17 @@
                 pass_piece(i).start()
             lend(step, j).wait_send()
             lend(step + 1, j).start()
+        elif ending:
+            for i in range(ENDS):
+                if last:
+                    end_piece(i).wait_recv()
+                each_tile(sizes[k], add, i * quarter // ROWS, quarter // ROWS)
+                if not last:
+                    end_piece(i).start()
         else:
             each_tile(sizes[k], add)
         if not last:
-            if not cut:
+            if not cut and not ending:
                 pass_on(step, j).start()
             get_own(step + 1, j).start()
         else:
@@ -218,10 +234,11 @@
     for r in range(ROWS // 8):
         for c in range(COLS // 128):
             mine = mine + acc[r * 8 : r * 8 + 8, c * 128 : c * 128 + 128]
-    totals[me] = mine
+    totals[me] = jnp.broadcast_to(jnp.sum(mine, axis=0, keepdims=True), (8, 128))
+    told = totals.at[me, pl.ds(0, 1)]
 
     def tell(i):
-        return remote(totals.at[me], totals.at[me], norm_s.at[i], norm_r.at[i], lax.rem(me + i, 16))
+        return remote(told, told, norm_s.at[i], norm_r.at[i], lax.rem(me + i, 16))
 
     for i in range(1, 16):
         tell(i).start()
@@ -231,9 +248,9 @@
             copy.wait()
     for i in range(1, 16):
         tell(i).wait()
-    total = totals[0]
+    total = totals[0, 0:1]
     for i in range(1, 16):
-        total = total + totals[i]
+        total = total + totals[i, 0:1]
     count = 16 * 2 * sum(rows * cols for rows, cols in sizes)
     factor_ref[...] = jnp.minimum(1.0, 0.5 * lax.rsqrt(jnp.full((8, 128), jnp.sum(total)) / count + 1e-30))
     factor = jnp.max(factor_ref[...])
@@ -337,6 +354,7 @@
             dma((16,)),
             dma((16,)),
             dma((sizes[0][0] // ROWS,)),
+            dma((ENDS,)),
         ],
         compiler_params=pltpu.CompilerParams(collective_id=0, has_side_effects=True, vmem_limit_bytes=VMEM_LIMIT),
         cost_estimate=pl.CostEstimate(flops=400_000_000, bytes_accessed=300_000_000, transcendentals=0),
@@ -407,10 +425,11 @@
     )(whole, *streams)
 
 
-def finish_kernel(layers, rows, _, came, given, out, store):
+def finish_kernel(layers, rows, whose, _, *refs):
+    *parts, out, store = refs
     copies = []
     for at, layer in enumerate(layers):
-        for mine, src in ((True, came), (False, given)):
+        for mine, src in zip(whose, parts, strict=True):
             dst = out.at[layer, rows_back(HOPS + 2, rows, mine)]
             copies.append(pltpu.make_async_copy(src.at[at], dst, store.at[len(copies)]))
     for copy in copies:
@@ -419,19 +438,19 @@
         copy.wait()
 
 
-def finish(layers, rows, w, came, given):
+def finish(layers, rows, w, whose, parts):
     hbm, vmem = pl.BlockSpec(memory_space=pltpu.HBM), pl.BlockSpec(memory_space=pltpu.VMEM)
     return pl.pallas_call(
-        functools.partial(finish_kernel, layers, rows),
+        functools.partial(finish_kernel, layers, rows, whose),
         out_shape=jax.ShapeDtypeStruct(w.shape, BF16),
-        in_specs=[hbm, vmem, vmem],
+        in_specs=[hbm] + [vmem] * len(parts),
         out_specs=hbm,
         input_output_aliases={0: 0},
-        scratch_shapes=[pltpu.SemaphoreType.DMA((2 * len(layers),))],
+        scratch_shapes=[pltpu.SemaphoreType.DMA((len(parts) * len(layers),))],
         compiler_params=pltpu.CompilerParams(vmem_limit_bytes=8 << 20),
-        cost_estimate=pl.CostEstimate(flops=8_000_000, bytes_accessed=came.size * 8, transcendentals=0),
+        cost_estimate=pl.CostEstimate(flops=8_000_000, bytes_accessed=parts[0].size * 8, transcendentals=0),
         name="finish",
-    )(w, came, given)
+    )(w, *parts)
 
 
 def permute(arrays, pairs):
@@ -460,7 +479,10 @@
             streams = [part[e] for e in mine for part in (edges, edge_given, came, given)]
             whole[k] = fill(k, one.shape[1], whole[k], streams)
         for e, (k, layers) in enumerate(STREAMS):
-            whole[k] = finish(layers, m[k].shape[1], whole[k], last[e], last_given[e])
+            both = [(True, last[e]), (False, last_given[e])]
+            groups = [[one] for one in both] if e == len(STREAMS) - 1 else [both]
+            for group in groups:
+                whole[k] = finish(layers, m[k].shape[1], whole[k], *(tuple(x) for x in zip(*group, strict=True)))
         return (*whole, *(one[0] for one in new), *(one[1] for one in new))
 
     all_of, cut = P(None, None, None), P(None, "dp", None)

time: 831 us -> 831 us (level)
  no operation moved by 1% of the time
where the time goes in v2:
time: 831 us; the launch traced here: 829 us
  Pallas kernels  710 us (85%)
  waiting for transfers between devices  87.3 us (11%)
  other arithmetic  16.2 us (2%)
  starting transfers between devices  11.2 us (1%)
    pallas_call x1, Pallas kernels, step_call(): pl.pallas_call(functools.partial(step_kernel, sizes), out_shape=[*arrays(...  650 us
    ppermute x20, waiting for transfers between devices, permute(): out.append(lax.ppermute(one, 'dp', pairs))  87.3 us
    pallas_call x3, Pallas kernels, fill(): pl.pallas_call(functools.partial(fill_kernel, k, rows), out_shape=jax.Sha...  50 us
  transfers between devices with their start and end apart: 20, of which 6 were waited for; matrix products, arithmetic and copies ran while one was open for 2% of the time, Pallas kernels for 7%

profile of v2, /device:TPU:0, one launch (start us, length us, event | category | flops | bytes accessed | tf_op | source)
XLA Modules:
  0.0 829.3 jit_solution(16475925933423604665)
XLA Ops:
  0.6 650.5 %step_kernel.1 = (bf16[2,80,5120]{2,1,0:T(8,128)(2,1)}, bf16[2,80,5120]{2,1,0:T(8,128)(2,1)}, bf16[2,320,1280]{2,1,0:T(8,128)(2,1)}, bf16[2,80,5120]{2,1,0:T(8,1...) custom-call(bf16[2,1280,5120]{2,1,0:T(8,128)(2,1)} %bitcast.4, ...), custom_call_target="tpu_custom_call" | custom-call | flops 400000000 | bytes 300000000 | tf_op jit(solution)/shard_map/step_kernel/pallas_call | solution.py:332
  651.1 1.5 collective-permute-start.11
  652.6 0.0 collective-permute-start.10
  652.6 0.6 collective-permute-start.14
  653.2 0.6 collective-permute-start.1
  653.8 1.5 collective-permute-start.6
  655.2 8.5 %collective-permute-done.11.refs_2_ = bf16[1,320,1280]{2,1,0:T(8,128)(2,1)S(1)} collective-permute-done((bf16[1,320,1280]{2,1,0:T(8,128)(2,1)}, bf16[1,320,1280]{2,1,0:T(8,128)(2,1)S(1)}, u32[]{:S(2)}, u32[]{:S(2)}) %collective-permute-start.11) | collective-permute-done | bytes 819232 | tf_op jit(solution)/shard_map/ppermute | solution.py:459
  663.8 0.0 collective-permute-start.13
  663.8 0.0 collective-permute-done.10.refs_1_
  663.8 0.0 copy-start.13
  663.8 1.5 collective-permute-start.16
  665.3 7.3 collective-permute-done.14.refs_6_
  672.5 0.0 collective-permute-start.12
  672.5 0.0 collective-permute-done.13.refs_5_
  672.5 1.5 collective-permute-start.18
  674.0 42.4 %collective-permute-done.16.refs_0_ = bf16[1,320,1280]{2,1,0:T(8,128)(2,1)S(1)} collective-permute-done((bf16[1,320,1280]{2,1,0:T(8,128)(2,1)S(1)}, bf16[1,320,1280]{2,1,0:T(8,128)(2,1)S(1)}, u32[]{:S(2)}, u32[]{:S(2)}) %collective-permute-start.16) | collective-permute-done | bytes 819232 | tf_op jit(solution)/shard_map/ppermute | solution.py:459
  716.4 0.5 collective-permute-start
  716.9 0.0 collective-permute-done.1.refs_2_
  716.9 1.5 collective-permute-start.3
  718.4 0.0 collective-permute-done.6.refs_2_
  718.4 0.6 collective-permute-start.8
  719.1 1.2 slice.3
  720.3 4.9 collective-permute-done.18.refs_0_
  725.2 0.5 collective-permute-start.19
  725.7 0.4 copy-done.17
  726.2 8.9 %fusion.2 = (f32[2,320,1280]{2,1,0:T(8,128)}, f32[2,320,1280]{2,1,0:T(8,128)}) fusion(f32[2,320,1280]{2,1,0:T(8,128)} %refs_11_.1, bf16[2,320,1280]{2,1,0:T(8,128)(2,1)} %get-tuple-element.30, f32[]{:T(128)} %bitcast.3, f32[2,320,1280]{2,1,0:T(8,128)} %refs_8_.1), kind=kLoop, calls=%fused_computation.5 | loop fusion | flops 7372800 | bytes 14745604 | tf_op jit(solution)/shard_map/add | solution.py:22
  735.1 0.0 copy-start.10
  735.1 0.5 collective-permute-start.5
  735.6 0.0 collective-permute-done.17.refs_1_
  735.6 0.1 collective-permute-start.2
  735.7 0.4 collective-permute-start.7
  736.1 6.6 collective-permute-done.3.refs_0_
  742.8 17.6 %collective-permute-done.8.refs_0_ = bf16[2,80,5120]{2,1,0:T(8,128)(2,1)S(1)} collective-permute-done((bf16[2,80,5120]{2,1,0:T(8,128)(2,1)}, bf16[2,80,5120]{2,1,0:T(8,128)(2,1)S(1)}, u32[]{:S(2)}, u32[]{:S(2)}) %collective-permute-start.8) | collective-permute-done | bytes 1638432 | tf_op jit(solution)/shard_map/ppermute | solution.py:459
  760.3 7.3 fusion
  767.6 16.7 %fill.5._ = bf16[2,5120,1280]{2,1,0:T(8,128)(2,1)} custom-call(bf16[2,5120,1280]{2,1,0:T(8,128)(2,1)} %get-tuple-element.24.whole, bf16[1,320,1280]{2,1,0:T(8,128)(2,1)} %get-tuple-element.25.refs_0_, bf16[1,320,1280]{2,1,0:T(8,128)(2,1)} %copy-done.13, bf16[1,320,1280]{2,1,0:T(8,128)(2,1)} %copy-done.12, bf16[1,320,1280]{2,1,0:T(8,128)(2,1)} %copy-done.16, ...), custom_call_target="tpu_custom_call" | custom-call | flops 60000000 | bytes 52428800 | tf_op jit(solution)/shard_map/fill/pallas_call | solution.py:412
  784.3 1.1 copy-done.1
  785.5 1.2 finish.7._
  786.7 0.5 copy-done.3
  787.2 0.9 finish.8._
  788.1 0.5 copy-done.5
  788.6 0.9 finish.9
  789.5 16.7 %fill.3._ = bf16[2,1280,5120]{2,1,0:T(8,128)(2,1)} custom-call(bf16[2,1280,5120]{2,1,0:T(8,128)(2,1)} %get-tuple-element.20.whole, bf16[2,80,5120]{2,1,0:T(8,128)(2,1)} %get-tuple-element.21.refs_0_, bf16[2,80,5120]{2,1,0:T(8,128)(2,1)} %copy-done.10, bf16[2,80,5120]{2,1,0:T(8,128)(2,1)} %collective-permute-done.1.refs_2_, ...), custom_call_target="tpu_custom_call" | custom-call | flops 60000000 | bytes 52428800 | tf_op jit(solution)/shard_map/fill/pallas_call | solution.py:412
  806.2 0.0 collective-permute-done.5.refs_1_
  806.2 0.0 collective-permute-done.7.refs_3_
  806.2 16.7 %fill.4._ = bf16[2,1280,5120]{2,1,0:T(8,128)(2,1)} custom-call(bf16[2,1280,5120]{2,1,0:T(8,128)(2,1)} %get-tuple-element.22.whole, bf16[2,80,5120]{2,1,0:T(8,128)(2,1)} %get-tuple-element.23.refs_0_, bf16[2,80,5120]{2,1,0:T(8,128)(2,1)} %collective-permute-done.5.refs_1_, bf16[2,80,5120]{2,1,0:T(8,128)(2,1)} %collective-permute-done.6.refs_2_, ...), custom_call_target="tpu_custom_call" | custom-call | flops 60000000 | bytes 52428800 | tf_op jit(solution)/shard_map/fill/pallas_call | solution.py:412
  822.9 0.0 collective-permute-done.4.refs_1_
  822.9 3.2 finish.5
  826.1 3.2 finish.6
  (40 shorter events, 0.1 us)
Async XLA Ops:
  651.1 12.6 %collective-permute-start.11 = (bf16[1,320,1280]{2,1,0:T(8,128)(2,1)}, bf16[1,320,1280]{2,1,0:T(8,128)(2,1)S(1)}, u32[]{:S(2)}, u32[]{:S(2)}) collective-permute-start(bf16[1,320,1280]{2,1,0:T(8,128)(2,1)} %get-tuple-element.25.refs_0_), channel_id=1, source_target_pairs={{0,2},{1,9},{2,4},{3,1},{4,6},{5,3},{6,14},{7,5},{8,0},{9,11},{10,... | collective-permute-start | bytes 2457608 | tf_op jit(solution)/shard_map/ppermute | solution.py:459
  652.6 11.1 %collective-permute-start.10 = (bf16[1,320,1280]{2,1,0:T(8,128)(2,1)}, bf16[1,320,1280]{2,1,0:T(8,128)(2,1)S(1)}, u32[]{:S(2)}, u32[]{:S(2)}) collective-permute-start(bf16[1,320,1280]{2,1,0:T(8,128)(2,1)} %get-tuple-element.25.refs_0_), channel_id=1, source_target_pairs={{0,1},{1,0},{2,3},{3,2},{4,5},{5,4},{6,7},{7,6},{8,9},{9,8},{10,11... | collective-permute-start | bytes 2457608 | tf_op jit(solution)/shard_map/ppermute | solution.py:459
  652.6 19.9 %collective-permute-start.14 = (bf16[1,320,1280]{2,1,0:T(8,128)(2,1)}, bf16[1,320,1280]{2,1,0:T(8,128)(2,1)S(1)}, u32[]{:S(2)}, u32[]{:S(2)}) collective-permute-start(bf16[1,320,1280]{2,1,0:T(8,128)(2,1)} %get-tuple-element.26.refs_4_), channel_id=1, source_target_pairs={{0,2},{1,9},{2,4},{3,1},{4,6},{5,3},{6,14},{7,5},{8,0},{9,11},{10,... | collective-permute-start | bytes 2457608 | tf_op jit(solution)/shard_map/ppermute | solution.py:459
  653.2 63.7 %collective-permute-start.1 = (bf16[2,80,5120]{2,1,0:T(8,128)(2,1)}, bf16[2,80,5120]{2,1,0:T(8,128)(2,1)}, u32[]{:S(2)}, u32[]{:S(2)}) collective-permute-start(bf16[2,80,5120]{2,1,0:T(8,128)(2,1)} %get-tuple-element.21.refs_0_), channel_id=1, source_target_pairs={{0,2},{1,9},{2,4},{3,1},{4,6},{5,3},{6,14},{7,5},{8,0},{9,11},{10,... | collective-permute-start | bytes 4915208 | tf_op jit(solution)/shard_map/ppermute | solution.py:459
  653.8 64.7 %collective-permute-start.6 = (bf16[2,80,5120]{2,1,0:T(8,128)(2,1)}, bf16[2,80,5120]{2,1,0:T(8,128)(2,1)}, u32[]{:S(2)}, u32[]{:S(2)}) collective-permute-start(bf16[2,80,5120]{2,1,0:T(8,128)(2,1)} %get-tuple-element.23.refs_0_), channel_id=1, source_target_pairs={{0,2},{1,9},{2,4},{3,1},{4,6},{5,3},{6,14},{7,5},{8,0},{9,11},{10,... | collective-permute-start | bytes 4915208 | tf_op jit(solution)/shard_map/ppermute | solution.py:459
  663.7 53.2 %copy-start.12 = (bf16[1,320,1280]{2,1,0:T(8,128)(2,1)}, bf16[1,320,1280]{2,1,0:T(8,128)(2,1)S(1)}, u32[]{:S(2)}) copy-start(bf16[1,320,1280]{2,1,0:T(8,128)(2,1)S(1)} %collective-permute-done.11.refs_2_) | copy-start | bytes 2457604
  663.8 8.8 %collective-permute-start.13 = (bf16[1,320,1280]{2,1,0:T(8,128)(2,1)}, bf16[1,320,1280]{2,1,0:T(8,128)(2,1)S(1)}, u32[]{:S(2)}, u32[]{:S(2)}) collective-permute-start(bf16[1,320,1280]{2,1,0:T(8,128)(2,1)} %get-tuple-element.26.refs_4_), channel_id=1, source_target_pairs={{0,1},{1,0},{2,3},{3,2},{4,5},{5,4},{6,7},{7,6},{8,9},{9,8},{10,11... | collective-permute-start | bytes 2457608 | tf_op jit(solution)/shard_map/ppermute | solution.py:459
  663.8 53.2 %copy-start.13 = (bf16[1,320,1280]{2,1,0:T(8,128)(2,1)}, bf16[1,320,1280]{2,1,0:T(8,128)(2,1)S(1)}, u32[]{:S(2)}) copy-start(bf16[1,320,1280]{2,1,0:T(8,128)(2,1)S(1)} %collective-permute-done.10.refs_1_) | copy-start | bytes 2457604
  663.8 52.6 %collective-permute-start.16 = (bf16[1,320,1280]{2,1,0:T(8,128)(2,1)S(1)}, bf16[1,320,1280]{2,1,0:T(8,128)(2,1)S(1)}, u32[]{:S(2)}, u32[]{:S(2)}) collective-permute-start(bf16[1,320,1280]{2,1,0:T(8,128)(2,1)S(1)} %collective-permute-done.11.refs_2_), channel_id=1, source_target_pairs={{0,2},{1,9},{2,4},{3,1},{4,6},{5,3},{6,14},{7,5},{8,0},{9,11},{10,... | collective-permute-start | bytes 2457608 | tf_op jit(solution)/shard_map/ppermute | solution.py:459
  672.5 53.2 %copy-start.14 = (bf16[1,320,1280]{2,1,0:T(8,128)(2,1)}, bf16[1,320,1280]{2,1,0:T(8,128)(2,1)S(1)}, u32[]{:S(2)}) copy-start(bf16[1,320,1280]{2,1,0:T(8,128)(2,1)S(1)} %collective-permute-done.14.refs_6_) | copy-start | bytes 2457604
  672.5 43.9 %collective-permute-start.12 = (bf16[1,320,1280]{2,1,0:T(8,128)(2,1)S(1)}, bf16[1,320,1280]{2,1,0:T(8,128)(2,1)S(1)}, u32[]{:S(2)}, u32[]{:S(2)}) collective-permute-start(bf16[1,320,1280]{2,1,0:T(8,128)(2,1)S(1)} %collective-permute-done.11.refs_2_), channel_id=1, source_target_pairs={{0,1},{1,0},{2,3},{3,2},{4,5},{5,4},{6,7},{7,6},{8,9},{9,8},{10,11... | collective-permute-start | bytes 2457608 | tf_op jit(solution)/shard_map/ppermute | solution.py:459
  672.5 45.9 %copy-start.15 = (bf16[1,320,1280]{2,1,0:T(8,128)(2,1)}, bf16[1,320,1280]{2,1,0:T(8,128)(2,1)S(1)}, u32[]{:S(2)}) copy-start(bf16[1,320,1280]{2,1,0:T(8,128)(2,1)S(1)} %collective-permute-done.13.refs_5_) | copy-start | bytes 2457604
  672.5 52.6 %collective-permute-start.18 = (bf16[1,320,1280]{2,1,0:T(8,128)(2,1)S(1)}, bf16[1,320,1280]{2,1,0:T(8,128)(2,1)S(1)}, u32[]{:S(2)}, u32[]{:S(2)}) collective-permute-start(bf16[1,320,1280]{2,1,0:T(8,128)(2,1)S(1)} %collective-permute-done.14.refs_6_), channel_id=1, source_target_pairs={{0,2},{1,9},{2,4},{3,1},{4,6},{5,3},{6,14},{7,5},{8,0},{9,11},{10,... | collective-permute-start | bytes 2457608 | tf_op jit(solution)/shard_map/ppermute | solution.py:459
  716.4 8.8 %collective-permute-start.15 = (bf16[1,320,1280]{2,1,0:T(8,128)(2,1)S(1)}, bf16[1,320,1280]{2,1,0:T(8,128)(2,1)S(1)}, u32[]{:S(2)}, u32[]{:S(2)}) collective-permute-start(bf16[1,320,1280]{2,1,0:T(8,128)(2,1)S(1)} %collective-permute-done.14.refs_6_), channel_id=1, source_target_pairs={{0,1},{1,0},{2,3},{3,2},{4,5},{5,4},{6,7},{7,6},{8,9},{9,8},{10,11... | collective-permute-start | bytes 2457608 | tf_op jit(solution)/shard_map/ppermute | solution.py:459
  716.4 2.0 copy-start.16
  716.4 18.6 %collective-permute-start = (bf16[2,80,5120]{2,1,0:T(8,128)(2,1)}, bf16[2,80,5120]{2,1,0:T(8,128)(2,1)S(1)}, u32[]{:S(2)}, u32[]{:S(2)}) collective-permute-start(bf16[2,80,5120]{2,1,0:T(8,128)(2,1)} %get-tuple-element.21.refs_0_), channel_id=1, source_target_pairs={{0,1},{1,0},{2,3},{3,2},{4,5},{5,4},{6,7},{7,6},{8,9},{9,8},{10,11... | collective-permute-start | bytes 4915208 | tf_op jit(solution)/shard_map/ppermute | solution.py:459
  716.9 25.8 %collective-permute-start.3 = (bf16[2,80,5120]{2,1,0:T(8,128)(2,1)}, bf16[2,80,5120]{2,1,0:T(8,128)(2,1)S(1)}, u32[]{:S(2)}, u32[]{:S(2)}) collective-permute-start(bf16[2,80,5120]{2,1,0:T(8,128)(2,1)} %collective-permute-done.1.refs_2_), channel_id=1, source_target_pairs={{0,2},{1,9},{2,4},{3,1},{4,6},{5,3},{6,14},{7,5},{8,0},{9,11},{10,... | collective-permute-start | bytes 4915208 | tf_op jit(solution)/shard_map/ppermute | solution.py:459
  718.4 41.9 %collective-permute-start.8 = (bf16[2,80,5120]{2,1,0:T(8,128)(2,1)}, bf16[2,80,5120]{2,1,0:T(8,128)(2,1)S(1)}, u32[]{:S(2)}, u32[]{:S(2)}) collective-permute-start(bf16[2,80,5120]{2,1,0:T(8,128)(2,1)} %collective-permute-done.6.refs_2_), channel_id=1, source_target_pairs={{0,2},{1,9},{2,4},{3,1},{4,6},{5,3},{6,14},{7,5},{8,0},{9,11},{10,... | collective-permute-start | bytes 4915208 | tf_op jit(solution)/shard_map/ppermute | solution.py:459
  725.2 9.9 %copy-start.2 = (bf16[1,320,1280]{2,1,0:T(8,128)(2,1)}, bf16[1,320,1280]{2,1,0:T(8,128)(2,1)S(1)}, u32[]{:S(2)}) copy-start(bf16[1,320,1280]{2,1,0:T(8,128)(2,1)S(1)} %collective-permute-done.18.refs_0_) | copy-start | bytes 2457604
  725.2 10.4 %collective-permute-start.17 = (bf16[1,320,1280]{2,1,0:T(8,128)(2,1)S(1)}, bf16[1,320,1280]{2,1,0:T(8,128)(2,1)S(1)}, u32[]{:S(2)}, u32[]{:S(2)}) collective-permute-start(bf16[1,320,1280]{2,1,0:T(8,128)(2,1)S(1)} %collective-permute-done.16.refs_0_), channel_id=1, source_target_pairs={{0,1},{1,0},{2,3},{3,2},{4,5},{5,4},{6,7},{7,6},{8,9},{9,8},{10,11... | collective-permute-start | bytes 2457608 | tf_op jit(solution)/shard_map/ppermute | solution.py:459
  725.2 1.0 copy-start.17
  725.2 10.5 %collective-permute-start.19 = (bf16[1,320,1280]{2,1,0:T(8,128)(2,1)S(1)}, bf16[1,320,1280]{2,1,0:T(8,128)(2,1)S(1)}, u32[]{:S(2)}, u32[]{:S(2)}) collective-permute-start(bf16[1,320,1280]{2,1,0:T(8,128)(2,1)S(1)} %collective-permute-done.18.refs_0_), channel_id=1, source_target_pairs={{0,1},{1,0},{2,3},{3,2},{4,5},{5,4},{6,7},{7,6},{8,9},{9,8},{10,11... | collective-permute-start | bytes 2457608 | tf_op jit(solution)/shard_map/ppermute | solution.py:459
  726.2 34.2 %copy-start.6 = (f32[2,80,5120]{2,1,0:T(8,128)S(1)}, f32[2,80,5120]{2,1,0:T(8,128)}, u32[]{:S(2)}) copy-start(f32[2,80,5120]{2,1,0:T(8,128)} %refs_6_.1) | copy-start | bytes 9830404
  726.2 34.2 %copy-start.7 = (f32[2,80,5120]{2,1,0:T(8,128)S(1)}, f32[2,80,5120]{2,1,0:T(8,128)}, u32[]{:S(2)}) copy-start(f32[2,80,5120]{2,1,0:T(8,128)} %refs_7_.1) | copy-start | bytes 9830404
  726.2 34.2 %copy-start.8 = (f32[2,80,5120]{2,1,0:T(8,128)S(1)}, f32[2,80,5120]{2,1,0:T(8,128)}, u32[]{:S(2)}) copy-start(f32[2,80,5120]{2,1,0:T(8,128)} %refs_9_.1) | copy-start | bytes 9830404
  726.2 34.2 %copy-start.9 = (f32[2,80,5120]{2,1,0:T(8,128)S(1)}, f32[2,80,5120]{2,1,0:T(8,128)}, u32[]{:S(2)}) copy-start(f32[2,80,5120]{2,1,0:T(8,128)} %refs_10_.1) | copy-start | bytes 9830404
  726.2 34.2 %copy-start.11 = (bf16[2,80,5120]{2,1,0:T(8,128)(2,1)S(1)}, bf16[2,80,5120]{2,1,0:T(8,128)(2,1)}, u32[]{:S(2)}) copy-start(bf16[2,80,5120]{2,1,0:T(8,128)(2,1)} %get-tuple-element.27) | copy-start | bytes 4915204
  735.1 32.6 %copy-start.10 = (bf16[2,80,5120]{2,1,0:T(8,128)(2,1)}, bf16[2,80,5120]{2,1,0:T(8,128)(2,1)S(1)}, u32[]{:S(2)}) copy-start(bf16[2,80,5120]{2,1,0:T(8,128)(2,1)S(1)} %collective-permute-done.refs_1_) | copy-start | bytes 4915204
  735.1 71.1 %collective-permute-start.5 = (bf16[2,80,5120]{2,1,0:T(8,128)(2,1)}, bf16[2,80,5120]{2,1,0:T(8,128)(2,1)}, u32[]{:S(2)}, u32[]{:S(2)}) collective-permute-start(bf16[2,80,5120]{2,1,0:T(8,128)(2,1)} %get-tuple-element.23.refs_0_), channel_id=1, source_target_pairs={{0,1},{1,0},{2,3},{3,2},{4,5},{5,4},{6,7},{7,6},{8,9},{9,8},{10,11... | collective-permute-start | bytes 4915208 | tf_op jit(solution)/shard_map/ppermute | solution.py:459
  735.6 32.0 %copy-start = (bf16[1,320,1280]{2,1,0:T(8,128)(2,1)}, bf16[1,320,1280]{2,1,0:T(8,128)(2,1)S(1)}, u32[]{:S(2)}) copy-start(bf16[1,320,1280]{2,1,0:T(8,128)(2,1)S(1)} %collective-permute-done.17.refs_1_) | copy-start | bytes 2457604
  735.6 53.9 %collective-permute-start.2 = (bf16[2,80,5120]{2,1,0:T(8,128)(2,1)}, bf16[2,80,5120]{2,1,0:T(8,128)(2,1)}, u32[]{:S(2)}, u32[]{:S(2)}) collective-permute-start(bf16[2,80,5120]{2,1,0:T(8,128)(2,1)} %collective-permute-done.1.refs_2_), channel_id=1, source_target_pairs={{0,1},{1,0},{2,3},{3,2},{4,5},{5,4},{6,7},{7,6},{8,9},{9,8},{10,11... | collective-permute-start | bytes 4915208 | tf_op jit(solution)/shard_map/ppermute | solution.py:459
  735.7 31.9 %copy-start.4 = (bf16[1,320,1280]{2,1,0:T(8,128)(2,1)}, bf16[1,320,1280]{2,1,0:T(8,128)(2,1)S(1)}, u32[]{:S(2)}) copy-start(bf16[1,320,1280]{2,1,0:T(8,128)(2,1)S(1)} %collective-permute-done.19.refs_0_) | copy-start | bytes 2457604
  735.7 70.5 %collective-permute-start.7 = (bf16[2,80,5120]{2,1,0:T(8,128)(2,1)}, bf16[2,80,5120]{2,1,0:T(8,128)(2,1)}, u32[]{:S(2)}, u32[]{:S(2)}) collective-permute-start(bf16[2,80,5120]{2,1,0:T(8,128)(2,1)} %collective-permute-done.6.refs_2_), channel_id=1, source_target_pairs={{0,1},{1,0},{2,3},{3,2},{4,5},{5,4},{6,7},{7,6},{8,9},{9,8},{10,11... | collective-permute-start | bytes 4915208 | tf_op jit(solution)/shard_map/ppermute | solution.py:459
  742.7 80.2 %collective-permute-start.4 = (bf16[2,80,5120]{2,1,0:T(8,128)(2,1)S(1)}, bf16[2,80,5120]{2,1,0:T(8,128)(2,1)}, u32[]{:S(2)}, u32[]{:S(2)}) collective-permute-start(bf16[2,80,5120]{2,1,0:T(8,128)(2,1)S(1)} %collective-permute-done.3.refs_0_), channel_id=1, source_target_pairs={{0,1},{1,0},{2,3},{3,2},{4,5},{5,4},{6,7},{7,6},{8,9},{9,8},{10,11... | collective-permute-start | bytes 4915208 | tf_op jit(solution)/shard_map/ppermute | solution.py:459
  760.3 65.8 %collective-permute-start.9 = (bf16[2,80,5120]{2,1,0:T(8,128)(2,1)S(1)}, bf16[2,80,5120]{2,1,0:T(8,128)(2,1)}, u32[]{:S(2)}, u32[]{:S(2)}) collective-permute-start(bf16[2,80,5120]{2,1,0:T(8,128)(2,1)S(1)} %collective-permute-done.8.refs_0_), channel_id=1, source_target_pairs={{0,1},{1,0},{2,3},{3,2},{4,5},{5,4},{6,7},{7,6},{8,9},{9,8},{10,11... | collective-permute-start | bytes 4915208 | tf_op jit(solution)/shard_map/ppermute | solution.py:459
  784.3 1.1 copy-start.1
  785.5 1.7 copy-start.3
  787.2 1.4 copy-start.5
